TPU v7x, 128 devices: a whole 4x4x4 slice. The times are simulated.
128 devices in a mesh: rep: 1, r: 16 (over y, z), s: 8 (over x, core).
Axes of the slice: x: 4, y: 4, z: 4, core: 2. Of those that a mesh axis runs over, the one named last changes fastest.
Arguments:
- x: bfloat16 [128, 2048, 1024], P(('rep', 'r', 's'))
- dy: bfloat16 [128, 2048, 1024], P(('rep', 'r', 's'))
- w_gate: bfloat16 [2, 1024, 4096], P(None, 's')
- w_up: bfloat16 [2, 1024, 4096], P(None, 's')
- w_down: bfloat16 [2, 4096, 1024], P(None, 's')
- m_w_gate: float32 [2, 1024, 4096], P(None, 's')
- m_w_up: float32 [2, 1024, 4096], P(None, 's')
- m_w_down: float32 [2, 4096, 1024], P(None, 's')
- v_w_gate: float32 [2, 1024, 4096], P(None, 's')
- v_w_up: float32 [2, 1024, 4096], P(None, 's')
- v_w_down: float32 [2, 4096, 1024], P(None, 's')
Outputs:
- output 1: bfloat16 [2, 1024, 4096], P('rep', 's')
- output 2: bfloat16 [2, 1024, 4096], P('rep', 's')
- output 3: bfloat16 [2, 4096, 1024], P('rep', 's')
- output 4: float32 [2, 1024, 4096], P('rep', 's')
- output 5: float32 [2, 1024, 4096], P('rep', 's')
- output 6: float32 [2, 4096, 1024], P('rep', 's')
- output 7: float32 [2, 1024, 4096], P('rep', 's')
- output 8: float32 [2, 1024, 4096], P('rep', 's')
- output 9: float32 [2, 4096, 1024], P('rep', 's')
All inputs are finite; a program needn't handle non-finite values.
Results may differ from a plain program's by a relative error of at most 0.022.
Values are sent between devices in bfloat16 or wider.
A program may use at most 1.5 GiB of HBM per device.

v0:
```python
import jax
import jax.numpy as jnp
from jax import lax
from jax.sharding import PartitionSpec as P

NAMES = ("w_gate", "w_up", "w_down")


def matmul(a, w):
    return jnp.dot(a, w, preferred_element_type=jnp.float32).astype(jnp.bfloat16)


def normed(h):
    wide = h.astype(jnp.float32)
    scale = lax.rsqrt(jnp.mean(wide**2, -1, keepdims=True) + 1e-6)
    return (wide * scale).astype(jnp.bfloat16)


def layer(h, w):
    a = normed(h)
    gate = jnp.dot(a, w["w_gate"], preferred_element_type=jnp.float32)
    up = jnp.dot(a, w["w_up"], preferred_element_type=jnp.float32)
    return h + matmul((jax.nn.silu(gate) * up).astype(jnp.bfloat16), w["w_down"])


def adamw(w, m, v, g):
    m = 0.9 * m + 0.1 * g
    v = 0.95 * v + 0.05 * g * g
    step = m * lax.rsqrt(v + 1e-8) + 0.1 * w
    return (w - 0.02 * step).astype(jnp.bfloat16), m, v


def solution(mesh):
    def fetched(weights, number):
        return {name: lax.all_gather(w[number], "s", axis=0, tiled=True) for name, w in zip(NAMES, weights, strict=True)}

    def summed(term):
        return lax.psum(lax.psum_scatter(term, "s", scatter_dimension=0, tiled=True), "r")

    def step(x, dy, *arrays):
        weights, m, v = (arrays[i : i + 3] for i in (0, 3, 6))
        layers = weights[0].shape[0]
        h, kept = x[0], []
        for number in range(layers):
            kept.append(h)
            h = layer(h, fetched(weights, number))
        by_h, mine = dy[0], [None] * layers
        for number in reversed(range(layers)):
            _, back = jax.vjp(lambda w, h: layer(h, w), fetched(weights, number), kept[number])
            by_w, by_h = back(by_h)
            mine[number] = [summed(by_w[name]) for name in NAMES]
        gradients = [jnp.stack([mine[number][i] for number in range(layers)]).astype(jnp.float32) for i in range(3)]
        new = [adamw(w.astype(jnp.float32), m, v, g) for w, m, v, g in zip(weights, m, v, gradients, strict=True)]
        return tuple(one[which] for which in range(3) for one in new)

    states, cut = P(("rep", "r", "s"), None, None), P(None, "s", None)
    return jax.shard_map(
        step,
        mesh=mesh,
        in_specs=(states, states) + (cut,) * 9,
        out_specs=(P("rep", "s", None),) * 9,
        check_vma=False,
    )
```

profile of v0, /device:TPU:1, one launch (start us, length us, event | category | flops | bytes accessed | tf_op | source)
XLA Modules:
  0.0 931.2 jit_solution(6144072236272162589)
XLA Ops:
  32.9 30.8 %all-gather.13.cloned.1.call-done = bf16[1,1024,4096]{2,1,0:T(8,128)(2,1)} async-done(((bf16[1,128,4096]{2,1,0:T(8,128)(2,1)}), bf16[1,1024,4096]{2,1,0:T(8,128)(2,1)}) %all-gather.13.cloned.1.call-update) | async-done | bytes 8388624 | tf_op jit(solution)/shard_map/all_gather | solution.py:35
  63.7 24.4 %fusion.35 = f32[2048,4096]{1,0:T(8,128)} fusion(bf16[1,1024,4096]{2,1,0:T(8,128)(2,1)} %all-gather.13.cloned.1.call-done, bf16[1,2048,1024]{1,2,0:T(8,128)(2,1)} %copy.20, f32[2048]{0:T(1024)S(1)} %add_rsqrt_fusion), kind=kOutput, calls=%fused_computation.53 | convolution fusion | flops 17186160640 | bytes 46145536 | tf_op jit(solution)/shard_map/dot_general | solution.py:21
  88.1 27.6 %all-gather.15.cloned.1.call-done = bf16[1,1024,4096]{2,1,0:T(8,128)(2,1)} async-done(((bf16[1,128,4096]{2,1,0:T(8,128)(2,1)}), bf16[1,1024,4096]{2,1,0:T(8,128)(2,1)}) %all-gather.15.cloned.1.call-update) | async-done | bytes 8388624 | tf_op jit(solution)/shard_map/all_gather | solution.py:35
  115.7 39.4 %multiply_convert_fusion.1 = (bf16[2048,4096]{1,0:T(8,128)(2,1)}, f32[2048,4096]{1,0:T(8,128)}) fusion(f32[2048,4096]{1,0:T(8,128)} %fusion.35, bf16[1,1024,4096]{2,1,0:T(8,128)(2,1)} %all-gather.15.cloned.1.call-done, bf16[1,2048,1024]{1,2,0:T(8,128)(2,1)} %copy.20, f32[2048]{0:T(1024)S(1)} %add_rsqrt_fusion), kind=kOutput, calls=%fused_computation.17 | convolution fusion | flops 17236492288 | bytes 96477184 | tf_op jit(solution)/shard_map/dot_general | solution.py:22
  167.8 24.5 %fusion.19 = (f32[2048]{0:T(1024)S(1)}, bf16[2048,1024]{0,1:T(8,128)(2,1)}) fusion(bf16[2048,4096]{1,0:T(8,128)(2,1)} %get-tuple-element.30, bf16[1,4096,1024]{2,1,0:T(8,128)(2,1)} %all-gather.17.cloned.1.call-done, bf16[1,2048,1024]{1,2,0:T(8,128)(2,1)} %copy.20), kind=kOutput, calls=%fused_computation.37 | convolution fusion | flops 17190352896 | bytes 33562624 | tf_op jit(solution)/shard_map/dot_general | solution.py:10
  192.9 26.8 %all-gather.23.cloned.1.call-done = bf16[1,1024,4096]{2,1,0:T(8,128)(2,1)} async-done(((bf16[1,128,4096]{2,1,0:T(8,128)(2,1)}), bf16[1,1024,4096]{2,1,0:T(8,128)(2,1)}) %all-gather.23.cloned.1.call-update) | async-done | bytes 8388624 | tf_op jit(solution)/shard_map/all_gather | solution.py:35
  219.7 24.4 %fusion.22 = f32[2048,4096]{1,0:T(8,128)} fusion(bf16[1,1024,4096]{2,1,0:T(8,128)(2,1)} %all-gather.23.cloned.1.call-done, bf16[2048,1024]{0,1:T(8,128)(2,1)} %get-tuple-element.33, f32[2048]{0:T(1024)S(1)} %fusion.74), kind=kOutput, calls=%fused_computation.40 | convolution fusion | flops 17186160640 | bytes 46145536 | tf_op jit(solution)/shard_map/jvp()/dot_general | solution.py:22
  244.1 27.5 %all-gather.21.cloned.1.call-done = bf16[1,4096,1024]{2,1,0:T(8,128)(2,1)} async-done(((bf16[1,512,1024]{2,1,0:T(8,128)(2,1)}), bf16[1,4096,1024]{2,1,0:T(8,128)(2,1)}) %all-gather.21.cloned.1.call-update) | async-done | bytes 8388624 | tf_op jit(solution)/shard_map/all_gather | solution.py:35
  271.6 24.4 %convolution_convert_fusion.1 = bf16[2048,4096]{1,0:T(8,128)(2,1)} fusion(bf16[1,4096,1024]{2,1,0:T(8,128)(2,1)} %all-gather.21.cloned.1.call-done, bf16[1,2048,1024]{2,1,0:T(8,128)(2,1)} %param.12), kind=kOutput, calls=%fused_computation.25 | convolution fusion | flops 17188257792 | bytes 29360128 | tf_op jit(solution)/shard_map/transpose(jvp())/dot_general | solution.py:10
  296.1 27.5 %all-gather.19.cloned.1.call-done = bf16[1,1024,4096]{2,1,0:T(8,128)(2,1)} async-done(((bf16[1,128,4096]{2,1,0:T(8,128)(2,1)}), bf16[1,1024,4096]{2,1,0:T(8,128)(2,1)}) %all-gather.19.cloned.1.call-update) | async-done | bytes 8388624 | tf_op jit(solution)/shard_map/all_gather | solution.py:35
  323.5 46.5 %fusion.2 = (bf16[2048,4096]{1,0:T(8,128)(2,1)}, f32[2048,4096]{1,0:T(8,128)}) fusion(f32[2048,4096]{1,0:T(8,128)} %fusion.22, bf16[2048,4096]{1,0:T(8,128)(2,1)} %convolution_convert_fusion.1, bf16[1,1024,4096]{2,1,0:T(8,128)(2,1)} %all-gather.19.cloned.1.call-done, bf16[2048,1024]{0,1:T(8,128)(2,1)} %get-tuple-element.33, f32[2048]{0:T(1024)S(1)} %fusion.74), kind=kOutput, calls=%fused_computation.8 | convolution fusion | flops 17286823936 | bytes 113254400 | tf_op jit(solution)/shard_map/jvp()/dot_general | solution.py:21
  370.0 27.3 %fusion.12 = bf16[2048,1024]{0,1:T(8,128)(2,1)} fusion(bf16[2048,4096]{1,0:T(8,128)(2,1)} %convolution_convert_fusion.1, bf16[1,1024,4096]{2,1,0:T(8,128)(2,1)} %all-gather.23.cloned.1.call-done, f32[2048,4096]{1,0:T(8,128)} %get-tuple-element.35), kind=kOutput, calls=%fused_computation.21 | convolution fusion | flops 17230200832 | bytes 62914560 | tf_op jit(solution)/shard_map/transpose(jvp())/dot_general | solution.py:22
  397.3 25.1 %fusion.21 = (f32[2048]{0:T(1024)S(1)}, bf16[2048,1024]{0,1:T(8,128)(2,1)S(1)}) fusion(bf16[2048,1024]{0,1:T(8,128)(2,1)S(1)} %copy-done.5, bf16[2048,1024]{0,1:T(8,128)(2,1)} %fusion.12, bf16[2048,4096]{1,0:T(8,128)(2,1)} %get-tuple-element.34, bf16[1,1024,4096]{2,1,0:T(8,128)(2,1)} %all-gather.19.cloned.1.call-done), kind=kOutput, calls=%fused_computation.39 | convolution fusion | flops 17190352896 | bytes 37756928 | tf_op jit(solution)/shard_map/transpose(jvp())/dot_general | solution.py:21
  427.6 23.2 %convolution_convert_fusion.2 = bf16[4096,1024]{1,0:T(8,128)(2,1)} fusion(bf16[2048,4096]{1,0:T(8,128)(2,1)} %get-tuple-element.30, bf16[2048,1024]{0,1:T(8,128)(2,1)S(1)} %fusion.59), kind=kOutput, calls=%fused_computation.59 | convolution fusion | flops 17184063488 | bytes 29360128 | tf_op jit(solution)/shard_map/transpose(jvp())/dot_general | solution.py:10
  450.9 30.6 %fusion.40 = bf16[4096,1024]{1,0:T(8,128)(2,1)} fusion(f32[2048,4096]{1,0:T(8,128)} %fusion.22, bf16[1,2048,1024]{2,1,0:T(8,128)(2,1)} %param.12, f32[2048,4096]{1,0:T(8,128)} %get-tuple-element.35), kind=kOutput, calls=%fused_computation.56 | convolution fusion | flops 17234395136 | bytes 79691776 | tf_op jit(solution)/shard_map/transpose(jvp())/dot_general | solution.py:10
  481.5 25.0 %convolution_convert_fusion = bf16[2048,4096]{1,0:T(8,128)(2,1)} fusion(bf16[2048,1024]{0,1:T(8,128)(2,1)} %copy-done.6, bf16[1,4096,1024]{2,1,0:T(8,128)(2,1)} %all-gather.17.cloned.1.call-done), kind=kOutput, calls=%fused_computation.24 | convolution fusion | flops 17188257792 | bytes 29360128 | tf_op jit(solution)/shard_map/transpose(jvp())/dot_general | solution.py:10
  506.5 27.0 %fusion.42 = bf16[1024,4096]{1,0:T(8,128)(2,1)} fusion(bf16[2048,4096]{1,0:T(8,128)(2,1)} %convolution_convert_fusion, f32[2048,4096]{1,0:T(8,128)} %fusion.35, bf16[1,2048,1024]{1,2,0:T(8,128)(2,1)} %copy.20, f32[2048]{0:T(1024)S(1)} %copy-done.15), kind=kOutput, calls=%fused_computation.58 | convolution fusion | flops 17240686592 | bytes 62922752 | tf_op jit(solution)/shard_map/transpose(jvp())/dot_general | solution.py:22
  534.1 26.7 %fusion.41 = bf16[1024,4096]{1,0:T(8,128)(2,1)} fusion(bf16[2048,4096]{1,0:T(8,128)(2,1)} %convolution_convert_fusion.1, bf16[2048,1024]{0,1:T(8,128)(2,1)} %get-tuple-element.33, f32[2048]{0:T(1024)S(1)} %copy-done.11, f32[2048,4096]{1,0:T(8,128)} %get-tuple-element.35), kind=kOutput, calls=%fused_computation.57 | convolution fusion | flops 17240686592 | bytes 62922752 | tf_op jit(solution)/shard_map/transpose(jvp())/dot_general | solution.py:22
  560.9 37.2 %fusion.37 = bf16[1024,4096]{1,0:T(8,128)(2,1)} fusion(f32[2048,4096]{1,0:T(8,128)} %fusion.35, f32[2048,4096]{1,0:T(8,128)} %get-tuple-element.31, bf16[2048,4096]{1,0:T(8,128)(2,1)} %convolution_convert_fusion, bf16[1,2048,1024]{1,2,0:T(8,128)(2,1)} %copy.20, f32[2048]{0:T(1024)S(1)} %copy-done.15), kind=kOutput, calls=%fused_computation.55 | convolution fusion | flops 17282629632 | bytes 96477184 | tf_op jit(solution)/shard_map/transpose(jvp())/dot_general | solution.py:21
  598.2 22.9 %convolution_convert_fusion.3 = bf16[1024,4096]{1,0:T(8,128)(2,1)} fusion(bf16[2048,4096]{1,0:T(8,128)(2,1)} %get-tuple-element.34, bf16[2048,1024]{0,1:T(8,128)(2,1)} %get-tuple-element.33, f32[2048]{0:T(1024)S(1)} %copy-done.11), kind=kOutput, calls=%fused_computation.60 | convolution fusion | flops 17186160640 | bytes 29368320 | tf_op jit(solution)/shard_map/transpose(jvp())/dot_general | solution.py:21
  621.3 45.3 %reduce-scatter.13.cloned.1.call-done = bf16[128,4096]{1,0:T(8,128)(2,1)} async-done(((bf16[1024,4096]{1,0:T(8,128)(2,1)}), bf16[128,4096]{1,0:T(8,128)(2,1)}) %reduce-scatter.13.cloned.1.call-update) | async-done | bytes 1048592 | tf_op jit(solution)/shard_map/reduce_scatter | solution.py:38
  666.6 54.6 %reduce-scatter.7.cloned.1.call-done = bf16[128,4096]{1,0:T(8,128)(2,1)} async-done(((bf16[1024,4096]{1,0:T(8,128)(2,1)}), bf16[128,4096]{1,0:T(8,128)(2,1)}) %reduce-scatter.7.cloned.1.call-update) | async-done | bytes 1048592 | tf_op jit(solution)/shard_map/reduce_scatter | solution.py:38
  721.2 54.5 %reduce-scatter.9.cloned.1.call-done = bf16[128,4096]{1,0:T(8,128)(2,1)} async-done(((bf16[1024,4096]{1,0:T(8,128)(2,1)}), bf16[128,4096]{1,0:T(8,128)(2,1)}) %reduce-scatter.9.cloned.1.call-update) | async-done | bytes 1048592 | tf_op jit(solution)/shard_map/reduce_scatter | solution.py:38
  775.7 126.6 %all-reduce.3.cloned.1.call-done = (bf16[1,128,4096]{2,1,0:T(8,128)(2,1)}, bf16[1,128,4096]{2,1,0:T(8,128)(2,1)}, bf16[1,128,4096]{2,1,0:T(8,128)(2,1)}, bf16[1,...) async-done(((bf16[1,128,4096]{2,1,0:T(8,128)(2,1)}, bf16[1,128,4096]{2,1,0:T(8,128)(2,1)}, bf16[1,128,4096]{2,1,0:T(8,128)(2,1)}, ...) | async-done | bytes 6291472 | tf_op jit(solution)/shard_map/psum | solution.py:38
  (74 shorter events, 67.0 us)
Async XLA Ops:
  7.2 56.5 %all-gather.13.cloned.1.call-start = ((), (), s32[]{:S(2)}) async-start(), calls=%async_computation.12 | async-start | bytes 9437184 | tf_op jit(solution)/shard_map/all_gather | solution.py:35
  10.5 105.3 %all-gather.15.cloned.1.call-start = ((), (), s32[]{:S(2)}) async-start(), calls=%async_computation.13 | async-start | bytes 9437184 | tf_op jit(solution)/shard_map/all_gather | solution.py:35
  13.6 154.2 %all-gather.17.cloned.1.call-start = ((), (), s32[]{:S(2)}) async-start(), calls=%async_computation.14 | async-start | bytes 9437184 | tf_op jit(solution)/shard_map/all_gather | solution.py:35
  15.2 204.5 %all-gather.23.cloned.1.call-start = ((), (), s32[]{:S(2)}) async-start(), calls=%async_computation.17 | async-start | bytes 9437184 | tf_op jit(solution)/shard_map/all_gather | solution.py:35
  15.8 255.8 %all-gather.21.cloned.1.call-start = ((), (), s32[]{:S(2)}) async-start(), calls=%async_computation.16 | async-start | bytes 9437184 | tf_op jit(solution)/shard_map/all_gather | solution.py:35
  16.4 307.2 %all-gather.19.cloned.1.call-start = ((), (), s32[]{:S(2)}) async-start(), calls=%async_computation.15 | async-start | bytes 9437184 | tf_op jit(solution)/shard_map/all_gather | solution.py:35
  16.9 604.3 %reduce-scatter.15.cloned.1.call-start = ((), (), s32[]{:S(2)}) async-start(), calls=%async_computation.10 | async-start | bytes 9437184 | tf_op jit(solution)/shard_map/reduce_scatter | solution.py:38
  26.5 89.2 %copy-start.14 = (f32[2048]{0:T(1024)}, f32[2048]{0:T(1024)S(1)}, u32[]{:S(2)}) copy-start(f32[2048]{0:T(1024)S(1)} %add_rsqrt_fusion) | copy-start | bytes 24580
  192.9 229.6 %copy-start.10 = (f32[2048]{0:T(1024)}, f32[2048]{0:T(1024)S(1)}, u32[]{:S(2)}) copy-start(f32[2048]{0:T(1024)S(1)} %fusion.74) | copy-start | bytes 24580
  370.0 27.3 %copy-start.5 = (bf16[2048,1024]{0,1:T(8,128)(2,1)S(1)}, bf16[2048,1024]{0,1:T(8,128)(2,1)}, u32[]{:S(2)}) copy-start(bf16[2048,1024]{0,1:T(8,128)(2,1)} %get-tuple-element.33) | copy-start | bytes 12582916
  397.3 25.1 %copy-start.13 = (f32[2048]{0:T(1024)S(1)}, f32[2048]{0:T(1024)}, u32[]{:S(2)}) copy-start(f32[2048]{0:T(1024)} %copy-done.12) | copy-start | bytes 24580
  397.3 25.2 %copy-start = (bf16[1,2048,1024]{1,2,0:T(8,128)(2,1)S(1)}, bf16[1,2048,1024]{1,2,0:T(8,128)(2,1)}, u32[]{:S(2)}) copy-start(bf16[1,2048,1024]{1,2,0:T(8,128)(2,1)} %copy.21) | copy-start | bytes 12582916
  450.8 170.4 %reduce-scatter.17.cloned.1.call-start = ((), (), s32[]{:S(2)}) async-start(), calls=%async_computation.11 | async-start | bytes 9437184 | tf_op jit(solution)/shard_map/reduce_scatter | solution.py:38
  481.5 25.0 %copy-start.15 = (f32[2048]{0:T(1024)S(1)}, f32[2048]{0:T(1024)}, u32[]{:S(2)}) copy-start(f32[2048]{0:T(1024)} %copy-done.14) | copy-start | bytes 24580
  481.5 139.8 %reduce-scatter.11.cloned.1.call-start = ((), (), s32[]{:S(2)}) async-start(), calls=%async_computation.8 | async-start | bytes 9437184 | tf_op jit(solution)/shard_map/reduce_scatter | solution.py:38
  533.5 133.1 %reduce-scatter.13.cloned.1.call-start = ((), (), s32[]{:S(2)}) async-start(), calls=%async_computation.9 | async-start | bytes 9437184 | tf_op jit(solution)/shard_map/reduce_scatter | solution.py:38
  560.9 160.3 %reduce-scatter.7.cloned.1.call-start = ((), (), s32[]{:S(2)}) async-start(), calls=%async_computation.6 | async-start | bytes 9437184 | tf_op jit(solution)/shard_map/reduce_scatter | solution.py:38
  598.2 177.4 %reduce-scatter.9.cloned.1.call-start = ((), (), s32[]{:S(2)}) async-start(), calls=%async_computation.7 | async-start | bytes 9437184 | tf_op jit(solution)/shard_map/reduce_scatter | solution.py:38
  621.1 281.1 %copy-start.4 = (bf16[2,512,1024]{2,1,0:T(8,128)(2,1)S(1)}, bf16[2,512,1024]{2,1,0:T(8,128)(2,1)}, u32[]{:S(2)}) copy-start(bf16[2,512,1024]{2,1,0:T(8,128)(2,1)} %param.15) | copy-start | bytes 6291460
  621.2 281.1 %all-reduce.3.cloned.1.call-start = ((), (), s32[]{:S(2)}) async-start(), calls=%async_computation.18 | async-start | bytes 12582912 | tf_op jit(solution)/shard_map/psum | solution.py:38
  902.2 8.7 copy-start.2
  902.2 8.7 copy-start.7
  902.2 8.7 copy-start.8
  902.3 8.7 copy-start.9
  (5 other events, 18.5 us)
Sparse Core Ops, SparseCore 0:
  10.6 53.0 all-gather.12
  66.0 49.7 all-gather.14
  118.0 49.7 all-gather.16
  170.0 49.7 all-gather.22
  221.9 49.7 all-gather.20
  273.8 49.7 all-gather.18
  451.0 51.8 reduce-scatter.14
  505.3 52.1 reduce-scatter.16
  559.9 52.1 reduce-scatter.10
  614.4 52.1 reduce-scatter.12
  669.0 52.1 reduce-scatter.6
  723.4 52.1 reduce-scatter.8
  779.9 122.3 all-reduce.2
where the time goes:
time: 941 us; the launch traced here: 931 us
  waiting for transfers between devices  436 us (46%)
  matrix products  429 us (46%)
  other arithmetic  28.1 us (3%)
  local copies, waits for them, and re-layouts  23.9 us (3%)
  between operations  14.6 us (2%)
    dot_general x5, matrix products, layer(): gate = jnp.dot(a, w['w_gate'], preferred_element_type=jnp.float32)  156 us
    reduce_scatter x6, waiting for transfers between devices, summed(): lax.psum_scatter(term, 's', scatter_dimension=0, tiled=True)  154 us
    all_gather x6, waiting for transfers between devices, fetched(): lax.all_gather(w[number], 's', axis=0, tiled=True)  153 us
    dot_general x5, matrix products, layer(): up = jnp.dot(a, w['w_up'], preferred_element_type=jnp.float32)  145 us
    dot_general x5, matrix products, matmul(): jnp.dot(a, w, preferred_element_type=jnp.float32).astype(jnp.bfloat16)  128 us
    psum x1, waiting for transfers between devices, summed(): lax.psum(lax.psum_scatter(term, 's', scatter_dimension=0, tiled=True), 'r')  127 us
    convert_element_type x2, other arithmetic, adamw(): return ((w - 0.02 * step).astype(jnp.bfloat16), m, v)  21.8 us
  transfers between devices with their start and end apart: 13, of which 10 were waited for; matrix products, arithmetic and copies ran while one was open for 35% of the time, Pallas kernels for 0%

commit v1 on v0

v1 whole, which is shorter than its diff:
```python
import functools

import jax
import jax.numpy as jnp
from jax import lax
from jax.experimental import pallas as pl
from jax.experimental.pallas import tpu as pltpu
from jax.sharding import Mesh
from jax.sharding import PartitionSpec as P

NAMES = ("w_gate", "w_up", "w_down")
BF, F32 = jnp.bfloat16, jnp.float32
MESH = pl.DeviceIdType.MESH
N4 = 4


def matmul(a, w):
    return jnp.dot(a, w, preferred_element_type=jnp.float32).astype(jnp.bfloat16)


def normed(h):
    wide = h.astype(jnp.float32)
    scale = lax.rsqrt(jnp.mean(wide**2, -1, keepdims=True) + 1e-6)
    return (wide * scale).astype(jnp.bfloat16)


def layer(h, w):
    a = normed(h)
    gate = jnp.dot(a, w["w_gate"], preferred_element_type=jnp.float32)
    up = jnp.dot(a, w["w_up"], preferred_element_type=jnp.float32)
    return h + matmul((jax.nn.silu(gate) * up).astype(jnp.bfloat16), w["w_down"])


def adamw(w, m, v, g):
    m = 0.9 * m + 0.1 * g
    v = 0.95 * v + 0.05 * g * g
    step = m * lax.rsqrt(v + 1e-8) + 0.1 * w
    return (w - 0.02 * step).astype(jnp.bfloat16), m, v


class Where:
    def __init__(self):
        self.x, self.y, self.z, self.c = (lax.axis_index(a) for a in ("x", "y", "z", "core"))

    def at(self, **by):
        out = {}
        for axis, d in by.items():
            mine = {"x": self.x, "y": self.y, "z": self.z, "core": self.c}[axis]
            n = 2 if axis == "core" else N4
            out[axis] = lax.rem(mine + d, n)
        return out


def greet(ids):
    barrier = pltpu.get_barrier_semaphore()
    for d in ids:
        pl.semaphore_signal(barrier, inc=1, device_id=d, device_id_type=MESH)
    pl.semaphore_wait(barrier, len(ids))


def x_partners(me):
    return [(dx, dc) for dx in range(N4) for dc in range(2) if (dx, dc) != (0, 0)]


def remote(src, dst, ss, rs, to):
    return pltpu.make_async_remote_copy(src_ref=src, dst_ref=dst, send_sem=ss, recv_sem=rs, device_id=to, device_id_type=MESH)


def gather_kernel(layers, wg, wu, wd, gf, uf, df, ssem, rsem, lsem):
    me = Where()
    greet([me.at(x=dx, core=dc) for dx, dc in x_partners(me)] + [me.at(y=d) for d in (1, 2, 3)] + [me.at(z=d) for d in (1, 2, 3)])
    xc = me.x * 2 + me.c
    rows = pl.ds(pl.multiple_of(32 * me.z, 32), 32)

    def cols(c, k):
        return pl.ds(pl.multiple_of(me.y * 1024 + c * 512 + k * 128, 128), 128)

    def first(l, k, q, go):
        for i, (w, f) in enumerate(((wg, gf), (wu, uf))):
            dst = f.at[l, k, me.y, xc, me.z]
            for n, (dx, dc) in enumerate(x_partners(me)):
                c = lax.rem(me.c + dc, 2)
                go(remote(w.at[l, rows, cols(c, k)], dst, ssem.at[q, i, n], rsem.at[q, i, n], me.at(x=dx, core=dc)))
            go(pltpu.make_async_copy(w.at[l, rows, cols(me.c, k)], dst, lsem.at[i]))
        src = wd.at[l, pl.ds(pl.multiple_of(128 * k, 128), 128)]
        for n, dx in enumerate((1, 2, 3)):
            go(remote(src, df.at[l, k, me.x], ssem.at[q, 2, n], rsem.at[q, 2, n], me.at(x=dx)))
        go(pltpu.make_async_copy(src, df.at[l, k, me.x], lsem.at[2]))

    def second(l, k, q, go):
        for n, d in enumerate((1, 2, 3)):
            v = gf.at[l, k, me.y, :, me.z]
            go(remote(v, v, ssem.at[q, 3, n], rsem.at[q, 3, n], me.at(y=d)))
            v = uf.at[l, k, me.y, :, me.z]
            go(remote(v, v, ssem.at[q, 4, n], rsem.at[q, 4, n], me.at(z=d)))

    def third(l, k, q, go):
        for n, d in enumerate((1, 2, 3)):
            v = gf.at[l, k, :, :, me.z]
            go(remote(v, v, ssem.at[q, 5, n], rsem.at[q, 5, n], me.at(z=d)))
            v = uf.at[l, k, me.y]
            go(remote(v, v, ssem.at[q, 6, n], rsem.at[q, 6, n], me.at(y=d)))

    def one(i, _):
        l, k, q = i // 4, i % 4, i % 2
        for stage in (first, second, third):
            stage(l, k, q, lambda c: c.start())
            stage(l, k, q, lambda c: c.wait())
        return 0

    lax.fori_loop(0, layers * 4, one, 0)


def gathered(wg, wu, wd):
    layers = wg.shape[0]
    any_ = pl.BlockSpec(memory_space=pl.ANY)
    return pl.pallas_call(
        functools.partial(gather_kernel, layers),
        out_shape=[
            jax.ShapeDtypeStruct((layers, 4, 4, 8, 4, 32, 128), BF),
            jax.ShapeDtypeStruct((layers, 4, 4, 8, 4, 32, 128), BF),
            jax.ShapeDtypeStruct((layers, 4, 4, 128, 1024), BF),
        ],
        in_specs=[any_] * 3,
        out_specs=[any_] * 3,
        scratch_shapes=[pltpu.SemaphoreType.DMA((2, 7, 8)), pltpu.SemaphoreType.DMA((2, 7, 8)), pltpu.SemaphoreType.DMA((3,))],
        compiler_params=pltpu.CompilerParams(collective_id=1, has_side_effects=True),
        name="gather",
    )(wg, wu, wd)


def solution(mesh):
    fine = Mesh(mesh.devices.reshape(4, 4, 4, 2), ("y", "z", "x", "core"))
    S = ("x", "core")
    R = ("y", "z")

    def summed(term):
        return lax.psum(lax.psum_scatter(term, S, scatter_dimension=0, tiled=True), R)

    def step(x, dy, *arrays):
        weights, m, v = (arrays[i : i + 3] for i in (0, 3, 6))
        layers = weights[0].shape[0]
        gf, uf, df = gathered(*weights)
        c = lax.axis_index("core")

        def both(f):
            o = lax.ppermute(f, "core", [(0, 1), (1, 0)])
            pair = jnp.where(c == 0, jnp.stack([f, o]), jnp.stack([o, f]))
            return pair.transpose(1, 4, 5, 6, 3, 0, 2, 7).reshape(layers, 1024, 4096)

        def rows(f):
            o = lax.ppermute(f, "core", [(0, 1), (1, 0)])
            pair = jnp.where(c == 0, jnp.stack([f, o]), jnp.stack([o, f]))
            return pair.transpose(1, 3, 0, 2, 4, 5).reshape(layers, 4096, 1024)

        whole = dict(zip(NAMES, (both(gf), both(uf), rows(df))))
        full = [{n: whole[n][l] for n in NAMES} for l in range(layers)]
        h, kept = x[0], []
        for number in range(layers):
            kept.append(h)
            h = layer(h, full[number])
        by_h, mine = dy[0], [None] * layers
        for number in reversed(range(layers)):
            _, back = jax.vjp(lambda w, h: layer(h, w), full[number], kept[number])
            by_w, by_h = back(by_h)
            mine[number] = [summed(by_w[name]) for name in NAMES]
        gradients = [jnp.stack([mine[number][i] for number in range(layers)]).astype(jnp.float32) for i in range(3)]
        new = [adamw(w.astype(jnp.float32), m, v, g) for w, m, v, g in zip(weights, m, v, gradients, strict=True)]
        return tuple(one[which] for which in range(3) for one in new)

    states, cut = P(("y", "z", "x", "core"), None, None), P(None, S, None)
    return jax.shard_map(
        step,
        mesh=fine,
        in_specs=(states, states) + (cut,) * 9,
        out_specs=(P(None, S, None),) * 9,
        check_vma=False,
    )
```

time: 941 us -> 1240 us (1.32)
  Pallas kernels: 0 us -> 263 us
  waiting for transfers between devices: 436 us -> 287 us
  local copies, waits for them, and re-layouts: 23.9 us -> 159 us
  other arithmetic: 28.1 us -> 73.5 us
    pallas_call x0 -> x1, Pallas kernels: none -> 263 us  [gathered(): pl.pallas_call(functools.partial(gather_kernel, layers), out_shape=[jax.S...]
    all_gather x6 -> x0, waiting for transfers between devices: 153 us -> none  [fetched(): lax.all_gather(w[number], 's', axis=0, tiled=True)]
    slice x3 -> x9, local copies, waits for them, and re-layouts: 7.78 us -> 81.3 us  [step(): full = [{n: whole[n][l] for n in NAMES} for l in range(layers)]]
    squeeze x0 -> x4, local copies, waits for them, and re-layouts: none -> 57.8 us  [step(): full = [{n: whole[n][l] for n in NAMES} for l in range(layers)]]
    transpose x0 -> x2, other arithmetic: none -> 44.4 us  [the longest x1 29 us: both(): return pair.transpose(1, 4, 5, 6, 3, 0, 2, 7).reshape(layers, 1024, 4096)]
  transfers between devices with their start and end apart: 13 -> 10, of which waited for: 10 -> 5; matrix products, arithmetic and copies ran while one was open for 35% -> 23% of each run, Pallas kernels for 0% -> 0%
where the time goes in v1:
time: 1240 us; the launch traced here: 1230 us
  matrix products  427 us (34%)
  waiting for transfers between devices  287 us (23%)
  Pallas kernels  263 us (21%)
  local copies, waits for them, and re-layouts  159 us (13%)
  other arithmetic  73.5 us (6%)
  between operations  14.5 us (1%)
    pallas_call x1, Pallas kernels, gathered(): pl.pallas_call(functools.partial(gather_kernel, layers), out_shape=[jax.S...  263 us
    dot_general x5, matrix products, layer(): gate = jnp.dot(a, w['w_gate'], preferred_element_type=jnp.float32)  155 us
    reduce_scatter x6, waiting for transfers between devices, summed(): lax.psum_scatter(term, S, scatter_dimension=0, tiled=True)  152 us
    dot_general x5, matrix products, layer(): up = jnp.dot(a, w['w_up'], preferred_element_type=jnp.float32)  144 us
    dot_general x5, matrix products, matmul(): jnp.dot(a, w, preferred_element_type=jnp.float32).astype(jnp.bfloat16)  128 us
    psum x1, waiting for transfers between devices, summed(): lax.psum(lax.psum_scatter(term, S, scatter_dimension=0, tiled=True), R)  127 us
    slice x9, local copies, waits for them, and re-layouts, step(): full = [{n: whole[n][l] for n in NAMES} for l in range(layers)]  81.3 us
    squeeze x4, local copies, waits for them, and re-layouts, step(): full = [{n: whole[n][l] for n in NAMES} for l in range(layers)]  57.8 us
  transfers between devices with their start and end apart: 10, of which 5 were waited for; matrix products, arithmetic and copies ran while one was open for 23% of the time, Pallas kernels for 0%

profile of v1, /device:TPU:1, one launch (start us, length us, event | category | flops | bytes accessed | tf_op | source)
XLA Modules:
  0.0 1229.2 jit_solution(1682633011641321410)
XLA Ops:
  7.2 263.0 %gather.1 = (bf16[2,4,4,8,4,32,128]{6,5,4,3,2,1,0:T(8,128)(2,1)}, bf16[2,4,4,8,4,32,128]{6,5,4,3,2,1,0:T(8,128)(2,1)}, bf16[2,4,4,128,1024]{4,3,2,1,0:T(8,128)(2,1)}) custom-call(bf16[2,128,4096]{2,1,0:T(8,128)(2,1)} %wg.1, bf16[2,128,4096]{2,1,0:T(8,128)(2,1)} %wu.1, bf16[2,512,1024]{2,1,0:T(8,128)(2,1)} %wd.1), custom_call_target="tpu_custom_call" | custom-call | tf_op jit(solution)/shard_map/gather/pallas_call | solution.py:117
  299.6 29.0 %fusion.14 = (bf16[2,8,4,32,4,2,4,128]{7,3,2,1,4,6,0,5:T(8,128)(2,1)S(1)}, bf16[2,8,4,32,4,2,4,128]{7,3,2,1,4,6,0,5:T(8,128)(2,1)}) fusion(bf16[1,2,4,4,8,4,32,128]{7,6,5,4,3,2,1,0:T(8,128)(2,1)} %bitcast.4, bf16[1,2,4,4,8,4,32,128]{7,6,5,4,3,2,1,0:T(8,128)(2,1)} %bitcast.69, pred[]{:T(512)S(6)} %eq.2, bf16[1,2,4,4,8,4,32,128]{7,6,5,4,3,2,1,0:T(8,128)(2,1)} %bitcast.70, ...), kind=kLoop, calls=%fused_computation.24 | loop fusion | flops 50331648 | bytes 67108864 | tf_op jit(solution)/shard_map/transpose | solution.py:149
  343.9 14.5 %squeeze.26 = bf16[1024,4096]{1,0:T(8,128)(2,1)} reshape(bf16[1,8,4,32,4,2,4,128]{7,6,5,4,3,2,1,0:T(4,128)(2,1)} %copy.25) | data formatting | bytes 16777216 | tf_op jit(solution)/shard_map/squeeze | solution.py:157
  391.3 15.4 %fusion.16 = bf16[2,4,2,4,128,1024]{5,4,1,3,0,2:T(8,128)(2,1)S(1)} fusion(bf16[1,2,4,4,128,1024]{5,4,3,2,1,0:T(8,128)(2,1)} %bitcast.10, bf16[1,2,4,4,128,1024]{5,4,3,2,1,0:T(8,128)(2,1)} %bitcast.68, pred[]{:T(512)S(6)} %eq.2), kind=kLoop, calls=%fused_computation.28 | loop fusion | flops 25165824 | bytes 33554432 | tf_op jit(solution)/shard_map/transpose | solution.py:154
  421.4 23.8 %fusion.61 = f32[2048,4096]{1,0:T(8,128)} fusion(bf16[1024,4096]{1,0:T(8,128)(2,1)} %squeeze.26, bf16[1,2048,1024]{2,1,0:T(8,128)(2,1)S(1)} %copy-done.6, f32[2048]{0:T(1024)S(1)} %add_rsqrt_fusion), kind=kOutput, calls=%fused_computation.92 | convolution fusion | flops 17186160640 | bytes 46145536 | tf_op jit(solution)/shard_map/dot_general | solution.py:29
  445.2 35.9 %multiply_convert_fusion.1 = (bf16[2048,4096]{1,0:T(8,128)(2,1)}, f32[2048,4096]{1,0:T(8,128)}) fusion(f32[2048,4096]{1,0:T(8,128)} %fusion.61, bf16[1024,4096]{1,0:T(8,128)(2,1)} %squeeze.27, bf16[1,2048,1024]{2,1,0:T(8,128)(2,1)} %param.11, f32[2048]{0:T(1024)S(1)} %add_rsqrt_fusion), kind=kOutput, calls=%fused_computation.17 | convolution fusion | flops 17236492288 | bytes 96477184 | tf_op jit(solution)/shard_map/dot_general | solution.py:30
  481.1 24.7 %fusion.22 = (f32[2048]{0:T(1024)S(1)}, bf16[2048,1024]{0,1:T(8,128)(2,1)}) fusion(bf16[2048,4096]{1,0:T(8,128)(2,1)} %get-tuple-element.36, bf16[4096,1024]{1,0:T(8,128)(2,1)} %bitcast.71, bf16[1,2048,1024]{1,2,0:T(8,128)(2,1)} %copy.23), kind=kOutput, calls=%fused_computation.43 | convolution fusion | flops 17190352896 | bytes 33562624 | tf_op jit(solution)/shard_map/dot_general | solution.py:18
  545.1 14.5 %squeeze.29 = bf16[1024,4096]{1,0:T(8,128)(2,1)} reshape(bf16[1,8,4,32,4,2,4,128]{7,6,5,4,3,2,1,0:T(4,128)(2,1)} %copy.28) | data formatting | bytes 16777216 | tf_op jit(solution)/shard_map/squeeze | solution.py:157
  568.0 24.6 %convolution_convert_fusion.1 = bf16[4096,2048]{0,1:T(8,128)(2,1)} fusion(bf16[4096,1024]{1,0:T(8,128)(2,1)} %bitcast.75, bf16[1,2048,1024]{2,1,0:T(8,128)(2,1)} %param.12), kind=kOutput, calls=%fused_computation.31 | convolution fusion | flops 17188257792 | bytes 29360128 | tf_op jit(solution)/shard_map/transpose(jvp())/dot_general | solution.py:18
  592.7 21.8 %fusion.55 = f32[2048,4096]{1,0:T(8,128)} fusion(bf16[1024,4096]{1,0:T(8,128)(2,1)S(1)} %bitcast.74, bf16[2048,1024]{0,1:T(8,128)(2,1)S(1)} %copy-done.4, f32[2048]{0:T(1024)S(1)} %fusion.63), kind=kOutput, calls=%fused_computation.86 | convolution fusion | flops 17186160640 | bytes 46145536 | tf_op jit(solution)/shard_map/jvp()/dot_general | solution.py:30
  614.5 46.8 %fusion.2 = (bf16[2048,4096]{1,0:T(8,128)(2,1)}, f32[2048,4096]{1,0:T(8,128)}) fusion(f32[2048,4096]{1,0:T(8,128)} %fusion.55, bf16[4096,2048]{0,1:T(8,128)(2,1)} %convolution_convert_fusion.1, bf16[1024,4096]{1,0:T(8,128)(2,1)} %squeeze.29, bf16[2048,1024]{0,1:T(8,128)(2,1)} %get-tuple-element.39, f32[2048]{0:T(1024)S(1)} %fusion.63), kind=kOutput, calls=%fused_computation.6 | convolution fusion | flops 17286823936 | bytes 113254400 | tf_op jit(solution)/shard_map/jvp()/dot_general | solution.py:29
  661.4 23.7 %fusion.78 = bf16[2048,1024]{0,1:T(8,128)(2,1)} fusion(bf16[2048,4096]{1,0:T(8,128)(2,1)} %get-tuple-element.40, bf16[1024,4096]{1,0:T(8,128)(2,1)} %squeeze.29), kind=kOutput, calls=%fused_computation.102 | convolution fusion | flops 17179869184 | bytes 29360128 | tf_op jit(solution)/shard_map/transpose(jvp())/dot_general | solution.py:29
  685.1 32.7 %fusion.24 = (f32[2048]{0:T(1024)S(1)}, bf16[2048,1024]{0,1:T(8,128)(2,1)}) fusion(bf16[2048,1024]{0,1:T(8,128)(2,1)} %get-tuple-element.39, bf16[2048,1024]{0,1:T(8,128)(2,1)} %fusion.78, bf16[1024,4096]{1,0:T(8,128)(2,1)} %squeeze.31, bf16[4096,2048]{0,1:T(8,128)(2,1)} %convolution_convert_fusion.1, f32[2048,4096]{1,0:T(8,128)} %get-tuple-element.41), kind=kOutput, calls=%fused_computation.45 | convolution fusion | flops 17242781696 | bytes 71311360 | tf_op jit(solution)/shard_map/transpose(jvp())/dot_general | solution.py:30
  725.2 23.1 %convolution_convert_fusion.2 = bf16[4096,1024]{1,0:T(8,128)(2,1)} fusion(bf16[2048,4096]{1,0:T(8,128)(2,1)} %get-tuple-element.36, bf16[2048,1024]{0,1:T(8,128)(2,1)S(1)} %fusion.48), kind=kOutput, calls=%fused_computation.51 | convolution fusion | flops 17184063488 | bytes 29360128 | tf_op jit(solution)/shard_map/transpose(jvp())/dot_general | solution.py:18
  748.5 30.6 %fusion.28 = bf16[4096,1024]{1,0:T(8,128)(2,1)} fusion(f32[2048,4096]{1,0:T(8,128)} %fusion.55, bf16[1,2048,1024]{2,1,0:T(8,128)(2,1)} %param.12, f32[2048,4096]{1,0:T(8,128)} %get-tuple-element.41), kind=kOutput, calls=%fused_computation.48 | convolution fusion | flops 17234395136 | bytes 79691776 | tf_op jit(solution)/shard_map/transpose(jvp())/dot_general | solution.py:18
  779.1 24.8 %convolution_convert_fusion = bf16[2048,4096]{1,0:T(8,128)(2,1)} fusion(bf16[2048,1024]{0,1:T(8,128)(2,1)} %copy-done.5, bf16[4096,1024]{1,0:T(8,128)(2,1)} %bitcast.72), kind=kOutput, calls=%fused_computation.30 | convolution fusion | flops 17188257792 | bytes 29360128 | tf_op jit(solution)/shard_map/transpose(jvp())/dot_general | solution.py:18
  803.9 27.2 %fusion.30 = bf16[1024,4096]{1,0:T(8,128)(2,1)} fusion(bf16[2048,4096]{1,0:T(8,128)(2,1)} %convolution_convert_fusion, f32[2048,4096]{1,0:T(8,128)} %fusion.61, bf16[1,2048,1024]{1,2,0:T(8,128)(2,1)} %copy.23, f32[2048]{0:T(1024)S(1)} %copy-done.20), kind=kOutput, calls=%fused_computation.50 | convolution fusion | flops 17240686592 | bytes 62922752 | tf_op jit(solution)/shard_map/transpose(jvp())/dot_general | solution.py:30
  831.8 26.8 %fusion.29 = bf16[1024,4096]{1,0:T(8,128)(2,1)} fusion(bf16[4096,2048]{0,1:T(8,128)(2,1)} %convolution_convert_fusion.1, bf16[2048,1024]{0,1:T(8,128)(2,1)} %get-tuple-element.39, f32[2048]{0:T(1024)S(1)} %copy-done.16, f32[2048,4096]{1,0:T(8,128)} %get-tuple-element.41), kind=kOutput, calls=%fused_computation.49 | convolution fusion | flops 17240686592 | bytes 62922752 | tf_op jit(solution)/shard_map/transpose(jvp())/dot_general | solution.py:30
  858.7 37.2 %fusion.25 = bf16[1024,4096]{1,0:T(8,128)(2,1)} fusion(f32[2048,4096]{1,0:T(8,128)} %fusion.61, f32[2048,4096]{1,0:T(8,128)} %get-tuple-element.37, bf16[2048,4096]{1,0:T(8,128)(2,1)} %convolution_convert_fusion, bf16[1,2048,1024]{1,2,0:T(8,128)(2,1)} %copy.23, f32[2048]{0:T(1024)S(1)} %copy-done.20), kind=kOutput, calls=%fused_computation.47 | convolution fusion | flops 17282629632 | bytes 96477184 | tf_op jit(solution)/shard_map/transpose(jvp())/dot_general | solution.py:29
  895.9 23.0 %convolution_convert_fusion.3 = bf16[1024,4096]{1,0:T(8,128)(2,1)} fusion(bf16[2048,4096]{1,0:T(8,128)(2,1)} %get-tuple-element.40, bf16[2048,1024]{0,1:T(8,128)(2,1)} %get-tuple-element.39, f32[2048]{0:T(1024)S(1)} %copy-done.16), kind=kOutput, calls=%fused_computation.52 | convolution fusion | flops 17186160640 | bytes 29368320 | tf_op jit(solution)/shard_map/transpose(jvp())/dot_general | solution.py:29
  919.1 43.2 %reduce-scatter.13.cloned.1.call-done = bf16[128,4096]{1,0:T(8,128)(2,1)} async-done(((bf16[1024,4096]{1,0:T(8,128)(2,1)}), bf16[128,4096]{1,0:T(8,128)(2,1)}) %reduce-scatter.13.cloned.1.call-update) | async-done | bytes 1048592 | tf_op jit(solution)/shard_map/reduce_scatter | solution.py:138
  962.3 54.5 %reduce-scatter.7.cloned.1.call-done = bf16[128,4096]{1,0:T(8,128)(2,1)} async-done(((bf16[1024,4096]{1,0:T(8,128)(2,1)}), bf16[128,4096]{1,0:T(8,128)(2,1)}) %reduce-scatter.7.cloned.1.call-update) | async-done | bytes 1048592 | tf_op jit(solution)/shard_map/reduce_scatter | solution.py:138
  1016.7 54.5 %reduce-scatter.9.cloned.1.call-done = bf16[128,4096]{1,0:T(8,128)(2,1)} async-done(((bf16[1024,4096]{1,0:T(8,128)(2,1)}), bf16[128,4096]{1,0:T(8,128)(2,1)}) %reduce-scatter.9.cloned.1.call-update) | async-done | bytes 1048592 | tf_op jit(solution)/shard_map/reduce_scatter | solution.py:138
  1071.2 126.5 %all-reduce.3.cloned.1.call-done = (bf16[1,128,4096]{2,1,0:T(8,128)(2,1)}, bf16[1,128,4096]{2,1,0:T(8,128)(2,1)}, bf16[1,128,4096]{2,1,0:T(8,128)(2,1)}, bf16[1,...) async-done(((bf16[1,128,4096]{2,1,0:T(8,128)(2,1)}, bf16[1,128,4096]{2,1,0:T(8,128)(2,1)}, bf16[1,128,4096]{2,1,0:T(8,128)(2,1)}, ...) | async-done | bytes 6291472 | tf_op jit(solution)/shard_map/psum | solution.py:138
  (91 shorter events, 172.9 us)
Async XLA Ops:
  7.2 911.8 %reduce-scatter.15.cloned.1.call-start = ((), (), s32[]{:S(2)}) async-start(), calls=%async_computation.10 | async-start | bytes 9437184 | tf_op jit(solution)/shard_map/reduce_scatter | solution.py:138
  270.2 21.0 %collective-permute-start = (bf16[2,4,4,8,4,32,128]{6,5,4,3,2,1,0:T(8,128)(2,1)}, bf16[2,4,4,8,4,32,128]{6,5,4,3,2,1,0:T(8,128)(2,1)}, u32[]{:S(2)}, u32[]{:S(2)}) collective-permute-start(bf16[2,4,4,8,4,32,128]{6,5,4,3,2,1,0:T(8,128)(2,1)} %get-tuple-element.12), channel_id=1, source_target_pairs={{0,1},{1,0},{2,3},{3,2},{4,5},{5,4},{6,7},{7,6},{8,9},{9,8},{10,11... | collective-permute-start | bytes 25165832 | tf_op jit(solution)/shard_map/ppermute | solution.py:147
  274.8 24.8 %collective-permute-start.1 = (bf16[2,4,4,8,4,32,128]{6,5,4,3,2,1,0:T(8,128)(2,1)}, bf16[2,4,4,8,4,32,128]{6,5,4,3,2,1,0:T(8,128)(2,1)}, u32[]{:S(2)}, u32[]{:S(2)}) collective-permute-start(bf16[2,4,4,8,4,32,128]{6,5,4,3,2,1,0:T(8,128)(2,1)} %get-tuple-element.13), channel_id=1, source_target_pairs={{0,1},{1,0},{2,3},{3,2},{4,5},{5,4},{6,7},{7,6},{8,9},{9,8},{10,11... | collective-permute-start | bytes 25165832 | tf_op jit(solution)/shard_map/ppermute | solution.py:147
  274.9 116.4 %collective-permute-start.2 = (bf16[2,4,4,128,1024]{4,3,2,1,0:T(8,128)(2,1)}, bf16[2,4,4,128,1024]{4,3,2,1,0:T(8,128)(2,1)}, u32[]{:S(2)}, u32[]{:S(2)}) collective-permute-start(bf16[2,4,4,128,1024]{4,3,2,1,0:T(8,128)(2,1)} %get-tuple-element.14), channel_id=1, source_target_pairs={{0,1},{1,0},{2,3},{3,2},{4,5},{5,4},{6,7},{7,6},{8,9},{9,8},{10,11... | collective-permute-start | bytes 25165832 | tf_op jit(solution)/shard_map/ppermute | solution.py:152
  291.2 154.0 %copy-start.19 = (f32[2048]{0:T(1024)}, f32[2048]{0:T(1024)S(1)}, u32[]{:S(2)}) copy-start(f32[2048]{0:T(1024)S(1)} %add_rsqrt_fusion) | copy-start | bytes 24580
  506.4 211.4 %copy-start.15 = (f32[2048]{0:T(1024)}, f32[2048]{0:T(1024)S(1)}, u32[]{:S(2)}) copy-start(f32[2048]{0:T(1024)S(1)} %fusion.63) | copy-start | bytes 24580
  559.6 33.1 %slice-start = ((s8[8388608]{0:T(1024)(128)(4,1)}), s8[4194304]{0:T(1024)(128)(4,1)S(1)}, s32[]{:S(2)}) async-start(s8[8388608]{0:T(1024)(128)(4,1)} %bitcast.73), calls=%async_computation.13 | async-start | bytes 8388608
  568.0 24.6 %slice-start.1 = ((s8[8388608]{0:T(1024)(128)(4,1)}), s8[4194304]{0:T(1024)(128)(4,1)S(1)}, s32[]{:S(2)}) async-start(s8[8388608]{0:T(1024)(128)(4,1)} %bitcast.73), calls=%async_computation.14 | async-start | bytes 8388608
  568.0 24.6 %copy-start.4 = (bf16[2048,1024]{0,1:T(8,128)(2,1)S(1)}, bf16[2048,1024]{0,1:T(8,128)(2,1)}, u32[]{:S(2)}) copy-start(bf16[2048,1024]{0,1:T(8,128)(2,1)} %get-tuple-element.39) | copy-start | bytes 12582916
  685.1 32.7 %copy-start.18 = (f32[2048]{0:T(1024)S(1)}, f32[2048]{0:T(1024)}, u32[]{:S(2)}) copy-start(f32[2048]{0:T(1024)} %copy-done.17) | copy-start | bytes 24580
  685.1 32.7 %copy-start = (bf16[1,2048,1024]{1,2,0:T(8,128)(2,1)S(1)}, bf16[1,2048,1024]{1,2,0:T(8,128)(2,1)}, u32[]{:S(2)}) copy-start(bf16[1,2048,1024]{1,2,0:T(8,128)(2,1)} %copy.24) | copy-start | bytes 12582916
  748.4 170.6 %reduce-scatter.17.cloned.1.call-start = ((), (), s32[]{:S(2)}) async-start(), calls=%async_computation.11 | async-start | bytes 9437184 | tf_op jit(solution)/shard_map/reduce_scatter | solution.py:138
  779.0 24.9 %copy-start.20 = (f32[2048]{0:T(1024)S(1)}, f32[2048]{0:T(1024)}, u32[]{:S(2)}) copy-start(f32[2048]{0:T(1024)} %copy-done.19) | copy-start | bytes 24580
  779.1 140.0 %reduce-scatter.11.cloned.1.call-start = ((), (), s32[]{:S(2)}) async-start(), calls=%async_computation.8 | async-start | bytes 9437184 | tf_op jit(solution)/shard_map/reduce_scatter | solution.py:138
  831.2 131.1 %reduce-scatter.13.cloned.1.call-start = ((), (), s32[]{:S(2)}) async-start(), calls=%async_computation.9 | async-start | bytes 9437184 | tf_op jit(solution)/shard_map/reduce_scatter | solution.py:138
  858.6 158.1 %reduce-scatter.7.cloned.1.call-start = ((), (), s32[]{:S(2)}) async-start(), calls=%async_computation.6 | async-start | bytes 9437184 | tf_op jit(solution)/shard_map/reduce_scatter | solution.py:138
  895.9 175.3 %reduce-scatter.9.cloned.1.call-start = ((), (), s32[]{:S(2)}) async-start(), calls=%async_computation.7 | async-start | bytes 9437184 | tf_op jit(solution)/shard_map/reduce_scatter | solution.py:138
  918.9 278.8 %copy-start.1 = (bf16[2,512,1024]{2,1,0:T(8,128)(2,1)S(1)}, bf16[2,512,1024]{2,1,0:T(8,128)(2,1)}, u32[]{:S(2)}) copy-start(bf16[2,512,1024]{2,1,0:T(8,128)(2,1)} %wd.1) | copy-start | bytes 6291460
  918.9 278.8 %all-reduce.3.cloned.1.call-start = ((), (), s32[]{:S(2)}) async-start(), calls=%async_computation.12 | async-start | bytes 12582912 | tf_op jit(solution)/shard_map/psum | solution.py:138
  1197.7 9.3 copy-start.2
  1197.7 9.3 copy-start.7
  1197.7 10.7 copy-start.8
  1197.7 10.9 copy-start.13
  1197.7 11.2 copy-start.14
  (9 other events, 47.9 us)
Sparse Core Ops, SparseCore 0:
  748.5 50.0 reduce-scatter.14
  801.0 52.1 reduce-scatter.16
  855.6 52.1 reduce-scatter.10
  910.1 52.1 reduce-scatter.12
  964.5 52.1 reduce-scatter.6
  1019.0 52.1 reduce-scatter.8
  1075.4 122.2 all-reduce.2

commit v2 on v0

v2 whole, which is shorter than its diff:
```python
import functools

import jax
import jax.numpy as jnp
from jax import lax
from jax.experimental import pallas as pl
from jax.experimental.pallas import tpu as pltpu
from jax.sharding import Mesh
from jax.sharding import PartitionSpec as P

BF, F32 = jnp.bfloat16, jnp.float32
MESH = pl.DeviceIdType.MESH
ANY = pl.BlockSpec(memory_space=pl.ANY)
DMA = pltpu.SemaphoreType.DMA
AXES = ("y", "z", "x", "core")
SIDE = 4
D, FF = 1024, 4096
OWN = 2048
TOKENS = 2 * OWN
CHUNKS = 4
WIDE = 512
TILE = 512
TILES = TOKENS // TILE
MINE = OWN // TILE
START, WAIT = (lambda c: c.start()), (lambda c: c.wait())
LANES, PART, QUARTER, SLOTS = 128, 32, 256, 8
SLICED = (SIDE, 8, SIDE, PART, LANES)
BLOCKS = (SIDE, LANES, D)


def nn(a, b):
    return lax.dot_general(a, b, (((1,), (0,)), ((), ())), preferred_element_type=F32)


def nt(a, b):
    return lax.dot_general(a, b, (((1,), (1,)), ((), ())), preferred_element_type=F32)


def tn(a, b):
    return lax.dot_general(a, b, (((0,), (0,)), ((), ())), preferred_element_type=F32)


def normed(h):
    wide = h.astype(F32)
    scale = lax.rsqrt(jnp.mean(wide**2, -1, keepdims=True) + 1e-6)
    return (wide * scale).astype(BF)


def sigmoid(g):
    return 0.5 * jnp.tanh(0.5 * g) + 0.5


def block(i, n):
    return pl.ds(pl.multiple_of(i * n, n), n)


def when(*conditions):
    return pl.when(functools.reduce(jnp.logical_and, conditions))


class Place:
    def __init__(self):
        self.x, self.y, self.z, self.core = (lax.axis_index(a) for a in ("x", "y", "z", "core"))
        self.xc = self.x * 2 + self.core

    def plus(self, **by):
        return {a: lax.rem(getattr(self, a) + d, 2 if a == "core" else SIDE) for a, d in by.items()}

    def along(self, axis, d):
        return lax.rem(getattr(self, axis) + d, SIDE)


ROW = [(dx, dc) for dx in range(SIDE) for dc in range(2) if (dx, dc) != (0, 0)]
OTHERS = (1, 2, 3)


def greet(me):
    ids = [me.plus(x=dx, core=dc) for dx, dc in ROW] + [me.plus(**{a: d}) for a in ("y", "z") for d in OTHERS]
    barrier = pltpu.get_barrier_semaphore()
    for d in ids:
        pl.semaphore_signal(barrier, inc=1, device_id=d, device_id_type=MESH)
    pl.semaphore_wait(barrier, len(ids))


def remote(src, dst, ss, rs, to):
    return pltpu.make_async_remote_copy(src_ref=src, dst_ref=dst, send_sem=ss, recv_sem=rs, device_id=to, device_id_type=MESH)


class Gather:
    BASE = (0, 14, 17, 23)
    SEMS = 29

    def __init__(self, me, w, f, sems):
        self.me, (self.wg, self.wu, self.wd), (self.gf, self.uf, self.df), (self.ss, self.rs, self.ls) = me, w, f, sems

    def _go(self, act, q, base, copies):
        for n, (src, dst, to) in enumerate(copies, self.BASE[base]):
            act(remote(src, dst, self.ss.at[q, n], self.rs.at[q, n], to))

    def first(self, act, l, k, slot, q):
        me = self.me
        rows = block(me.z, PART)
        both = (self.wg, self.gf.at[slot, me.y, me.xc, me.z]), (self.wu, self.uf.at[slot, me.y, me.xc, me.z])

        def cols(c):
            return block((me.y * 2 + c) * CHUNKS + k, LANES)

        self._go(act, q, 0, [(w.at[l, rows, cols(lax.rem(me.core + dc, 2))], to, me.plus(x=dx, core=dc)) for dx, dc in ROW for w, to in both])
        for i, (w, to) in enumerate(both):
            act(pltpu.make_async_copy(w.at[l, rows, cols(me.core)], to, self.ls.at[q, i]))

    def down(self, act, l, k, slot, q):
        src, dst = self.wd.at[l, block(k, LANES)], self.df.at[slot, self.me.x]
        self._go(act, q, 1, [(src, dst, self.me.plus(x=d)) for d in OTHERS])
        act(pltpu.make_async_copy(src, dst, self.ls.at[q, 2]))

    def second(self, act, slot, q):
        me = self.me
        g, u = (f.at[slot, me.y, :, me.z] for f in (self.gf, self.uf))
        self._go(act, q, 2, [c for d in OTHERS for c in ((g, g, me.plus(y=d)), (u, u, me.plus(z=d)))])

    def third(self, act, slot, q):
        me = self.me
        g, u = self.gf.at[slot, :, :, me.z], self.uf.at[slot, me.y]
        self._go(act, q, 3, [c for d in OTHERS for c in ((g, g, me.plus(z=d)), (u, u, me.plus(y=d)))])

    def load(self, act, slot, v, sem):
        load(act, (self.gf, self.uf, self.df), slot, v, sem)


def load(act, f, slot, v, sem):
    src, to = slot
    for i in range(3):
        act(pltpu.make_async_copy(f[i].at[src], v[i].at[to], sem.at[i]))


def gather_scratch(chunks):
    return [DMA((chunks, Gather.SEMS)), DMA((chunks, Gather.SEMS)), DMA((chunks, 3))]


def matrix(v, slot):
    return jnp.concatenate([v[slot, u].reshape(D, LANES) for u in range(SIDE)], axis=1)


class Reduce:
    BASE = (0, 9, 18, 35, 44)
    SEMS = (2, 53)

    @staticmethod
    def scratch():
        v = pltpu.VMEM
        held = lambda *s: v(s, BF)
        came = lambda *s: v((2, 3) + s, BF)
        return [
            held(*SLICED), held(*SLICED), held(*BLOCKS),
            came(8, SIDE, PART, LANES), came(SIDE, 8, PART, LANES), came(LANES, D),
            held(8, SIDE, PART, LANES), held(SIDE, 8, PART, LANES), held(LANES, D),
            came(8, PART, LANES), came(8, PART, LANES), came(PART, D),
            held(8, PART, LANES), held(8, PART, LANES), held(PART, D),
            v((2, 8, PART, LANES), BF), v((2, 8, PART, LANES), BF), came(PART, QUARTER),
            held(2, PART, LANES), held(2, PART, LANES), held(PART, QUARTER),
            DMA(Reduce.SEMS), DMA(Reduce.SEMS), DMA((2, 3)),
        ]

    def __init__(self, me, scratch, out):
        self.me, self.out = me, out
        self.w, self.r1, self.b1, self.r2, self.b2, self.r3, self.b3 = (scratch[3 * i : 3 * i + 3] for i in range(7))
        self.ss, self.rs, self.ls = scratch[-3:]

    def put(self, g, u, d):
        for w, acc in ((self.w[0], g), (self.w[1], u)):
            for i in range(SIDE):
                w[i] = acc[:, LANES * i : LANES * (i + 1)].astype(BF).reshape(8, SIDE, PART, LANES)
        self.w[2][...] = d[...].astype(BF).reshape(BLOCKS)

    def copies(self, stage, slot, q):
        me = self.me
        (g, u, d), row = self.out, block(me.y, PART)
        if stage == 1:
            for n, by in enumerate(OTHERS):
                y, z, x = (me.along(a, by) for a in ("y", "z", "x"))
                yield self.w[0].at[y], self.r1[0].at[q, n], me.plus(y=by)
                yield self.w[1].at[:, :, z], self.r1[1].at[q, n], me.plus(z=by)
                yield self.w[2].at[x], self.r1[2].at[q, n], me.plus(x=by)
        elif stage == 2:
            for n, by in enumerate(OTHERS):
                y, z = (me.along(a, by) for a in ("y", "z"))
                yield self.b1[0].at[:, z], self.r2[0].at[q, n], me.plus(z=by)
                yield self.b1[1].at[y], self.r2[1].at[q, n], me.plus(y=by)
                yield self.b1[2].at[block(y, PART)], self.r2[2].at[q, n], me.plus(y=by)
        elif stage == 3:
            for dx, dc in ROW:
                x, c = me.along("x", dx), lax.rem(me.core + dc, 2)
                for i in range(2):
                    yield self.b2[i].at[2 * x + c], self.r3[i].at[q, me.xc], me.plus(x=dx, core=dc)
            for n, by in enumerate(OTHERS):
                cols = block(me.along("z", by), QUARTER)
                yield self.b2[2].at[:, cols], self.r3[2].at[q, n], me.plus(z=by)
        elif stage == 4:
            for by in OTHERS:
                yield self.b3[0], g.at[slot, :, me.y, me.z], me.plus(z=by)
                yield self.b3[1], u.at[slot, :, me.y, me.z], me.plus(y=by)
                yield self.b3[2], d.at[slot, row, block(me.z, QUARTER)], me.plus(z=by)
        else:
            for by in OTHERS:
                yield g.at[slot, :, me.y], g.at[slot, :, me.y], me.plus(y=by)
                yield u.at[slot, :, :, me.z], u.at[slot, :, :, me.z], me.plus(z=by)
                yield d.at[slot, row], d.at[slot, row], me.plus(y=by)

    def send(self, stage, act, slot, q):
        me = self.me
        for n, (src, dst, to) in enumerate(self.copies(stage, slot, q)):
            n += self.BASE[stage - 1]
            act(remote(src, dst, self.ss.at[q, n], self.rs.at[q, n], to))
        if stage == SIDE:
            g, u, d = self.out
            ends = g.at[slot, :, me.y, me.z], u.at[slot, :, me.y, me.z], d.at[slot, block(me.y, PART), block(me.z, QUARTER)]
            for i, dst in enumerate(ends):
                act(pltpu.make_async_copy(self.b3[i], dst, self.ls.at[q, i]))

    def add(self, stage, q):
        me = self.me
        cols = block(me.z, QUARTER)
        if stage == 3:
            for r, b, own in zip(self.r3[:2], self.b3, self.b2):
                r[q, me.xc] = own[me.xc]
                for c in range(2):
                    total = r[q, c].astype(F32)
                    for x in OTHERS:
                        total += r[q, 2 * x + c].astype(F32)
                    b[c] = total.astype(BF)
            parts = ((self.b2[2].at[:, cols], self.r3[2], self.b3[2]),)
        elif stage == 2:
            own = self.b1[0].at[:, me.z], self.b1[1].at[me.y], self.b1[2].at[block(me.y, PART)]
            parts = zip(own, self.r2, self.b2)
        else:
            own = self.w[0].at[me.y], self.w[1].at[:, :, me.z], self.w[2].at[me.x]
            parts = zip(own, self.r1, self.b1)
        for own, r, b in parts:
            total = own[...].astype(F32)
            for n in range(3):
                total += r[q, n].astype(F32)
            b[...] = total.astype(BF)

    def turn(self, stage, slot, q):
        self.send(stage, WAIT, slot, q)
        if stage < SIDE:
            self.add(stage, q)
        self.send(stage + 1, START, slot, q)


def reduced_shapes(n):
    s = jax.ShapeDtypeStruct((n, 2, SIDE, SIDE, PART, LANES), BF)
    return [s, s, jax.ShapeDtypeStruct((n, LANES, D), BF)]


def gathered_shapes(n):
    s = jax.ShapeDtypeStruct((n,) + SLICED, BF)
    return [s, s, jax.ShapeDtypeStruct((n,) + BLOCKS, BF)]


def chunk_buffers():
    return [pltpu.VMEM((2,) + SLICED, BF)] * 2 + [pltpu.VMEM((2,) + BLOCKS, BF)]


def tile_of(i):
    k, t = i // TILES, i % TILES
    return jnp.where(k == CHUNKS - 1, (t + MINE) % TILES, t)


def rows_of(tile):
    return block(tile, TILE)


def params(collective_id):
    return pltpu.CompilerParams(collective_id=collective_id, has_side_effects=True, vmem_limit_bytes=66_000_000, dimension_semantics=("arbitrary",))


def forward_kernel(x, dy, wg, wu, wd, g_out, u_out, a_out, h_out, n_out, dyp, gf, uf, df, a, xv, acc, prt, vg, vu, vd, ss, rs, ls, wsem, csem, esem, psem):
    i = pl.program_id(0)
    k, t = i // TILES, i % TILES
    me = Place()
    ga = Gather(me, (wg, wu, wd), (gf, uf, df), (ss, rs, ls))
    v = (vg, vu, vd)
    other = me.plus(core=1)
    mine, theirs = pl.ds(0, OWN), pl.ds(OWN, OWN)
    to_dy = remote(dy, dyp, esem.at[0], esem.at[1], other)
    to_a = remote(a.at[mine], a.at[theirs], esem.at[2], esem.at[3], other)
    save_a = pltpu.make_async_copy(a, a_out, csem.at[0])

    def spread(m, act, stage):
        if stage in ("first", "down"):
            getattr(ga, stage)(act, m // CHUNKS, m % CHUNKS, m, m)
        else:
            getattr(ga, stage)(act, m, m)

    def part(tile):
        return remote(acc.at[rows_of(tile)], prt.at[rows_of(tile - MINE)], psem.at[0, tile - MINE], psem.at[1, tile - MINE], other)

    @pl.when(i == 0)
    def _():
        fetch = pltpu.make_async_copy(x, xv, csem.at[1])
        fetch.start()
        greet(me)
        for m in range(3):
            spread(m, START, "first")
        spread(0, START, "down")
        fetch.wait()

        def norm(j, _):
            r = block(j, QUARTER)
            a[r] = normed(xv[r])
            return 0

        lax.fori_loop(0, OWN // QUARTER, norm, 0)
        spread(0, WAIT, "first")
        spread(0, START, "second")
        to_a.start()
        spread(0, WAIT, "second")
        spread(0, START, "third")
        spread(1, WAIT, "first")
        spread(1, START, "second")
        spread(0, WAIT, "third")
        spread(0, WAIT, "down")
        ga.load(START, (0, 0), v, wsem)

    @pl.when(t == 0)
    def _():
        ga.load(WAIT, (k, k % 2), v, wsem)
        spread(k + 1, WAIT, "second")
        spread(k + 1, START, "third")
        spread(k + 1, START, "down")

        @pl.when(k < 3)
        def _():
            spread(k + 2, WAIT, "first")
            spread(k + 2, START, "second")

        @pl.when(k < 2)
        def _():
            spread(k + 3, START, "first")

    @pl.when(i == MINE)
    def _():
        to_a.wait()
        save_a.start()
        to_dy.start()

    @when(t == TILES - 1, k < CHUNKS - 1)
    def _():
        spread(k + 1, WAIT, "third")
        spread(k + 1, WAIT, "down")
        ga.load(START, (k + 1, (k + 1) % 2), v, wsem)

    @when(k == CHUNKS - 1, t >= 1, t <= MINE)
    def _():
        part(t - 1 + MINE).start()

    tile = tile_of(i)
    rows = rows_of(tile)
    s = k % 2
    at = a[rows]
    g = nn(at, matrix(vg, s))
    u = nn(at, matrix(vu, s))
    g_out[0] = g
    u_out[0] = u
    hidden = (g * sigmoid(g) * u).astype(BF)
    acc[rows] = jnp.where(k == 0, 0.0, acc[rows]) + nn(hidden, vd[s].reshape(WIDE, D))

    @pl.when(i == CHUNKS * TILES - 1)
    def _():
        save_a.wait()
        for j in range(MINE):
            part(MINE + j).wait()

        def end(j, _):
            r = block(j, QUARTER)
            h = (xv[r].astype(F32) + (acc[r] + prt[r]).astype(BF).astype(F32)).astype(BF)
            xv[r] = h
            a[r] = normed(h)
            return 0

        lax.fori_loop(0, OWN // QUARTER, end, 0)
        keep = pltpu.make_async_copy(xv, h_out, csem.at[1])
        keep2 = pltpu.make_async_copy(a.at[mine], n_out, csem.at[2])
        keep.start()
        keep2.start()
        to_dy.wait()
        spread(CHUNKS, WAIT, "third")
        spread(CHUNKS, WAIT, "down")
        keep.wait()
        keep2.wait()


def forward(x, dy, weights):
    steps = CHUNKS * TILES
    wide = pl.BlockSpec((1, TILE, WIDE), lambda i: (i // TILES, tile_of(i), 0))
    big = jax.ShapeDtypeStruct((CHUNKS, TOKENS, WIDE), F32)
    own = jax.ShapeDtypeStruct((OWN, D), BF)
    return pl.pallas_call(
        forward_kernel,
        grid=(steps,),
        in_specs=[ANY] * 5,
        out_specs=[wide, wide] + [ANY] * 7,
        out_shape=[big, big, jax.ShapeDtypeStruct((TOKENS, D), BF), own, own, own] + gathered_shapes(CHUNKS + 1),
        scratch_shapes=[
            pltpu.VMEM((TOKENS, D), BF), pltpu.VMEM((OWN, D), BF), pltpu.VMEM((TOKENS, D), F32), pltpu.VMEM((OWN, D), F32),
            *chunk_buffers(), *gather_scratch(CHUNKS + 1), DMA((3,)), DMA((3,)), DMA((4,)), DMA((2, MINE)),
        ],
        compiler_params=params(1),
        name="forward",
    )(x, dy, *weights)


def gradients_of(g, u, dh):
    s = sigmoid(g)
    si = g * s
    return (si * u).astype(BF), (dh * u * (s + si * (1 - s))).astype(BF), (dh * si).astype(BF)


def middle_kernel(dy, dyp, n, g4, u4, d4, wg, wu, wd, dao, dar, rg, ru, rd, kg, ku, kd, gf, uf, df, *scratch):
    a, da, ag, au, ad, vg, vu, vd, ss, rs, ls, wsem, csem, esem, psem, *rest = scratch
    i = pl.program_id(0)
    k, t = i // TILES, i % TILES
    me = Place()
    ga = Gather(me, (wg, wu, wd), (gf, uf, df), (ss, rs, ls))
    re = Reduce(me, rest, (rg, ru, rd))
    v = (vg, vu, vd)
    other = me.plus(core=1)
    mine, theirs = block(0, OWN), block(1, OWN)
    to_a = remote(n, a.at[theirs], esem.at[0], esem.at[1], other)
    last = CHUNKS - 1

    def part(tile):
        return remote(da.at[rows_of(tile)], dar.at[rows_of(tile - MINE)], psem.at[0, tile - MINE], psem.at[1, tile - MINE], other)

    def keep(tile):
        return pltpu.make_async_copy(da.at[rows_of(tile)], dao.at[rows_of(tile)], csem.at[tile])

    def bring(stage, act, c):
        if stage in ("first", "down"):
            getattr(ga, stage)(act, 1, c + 1, c, c)
        else:
            getattr(ga, stage)(act, c, c)

    @when(i == 0)
    def _():
        fetch = pltpu.make_async_copy(n, a.at[mine], csem.at[0])
        fetch.start()
        load(START, (g4, u4, d4), (CHUNKS, 0), v, wsem)
        greet(me)
        to_a.start()
        for c in range(last):
            bring("first", START, c)
        bring("down", START, 0)
        fetch.wait()
        load(WAIT, (g4, u4, d4), (CHUNKS, 0), v, wsem)

    @when(t == 0, k > 0)
    def _():
        ga.load(WAIT, (k - 1, k % 2), v, wsem)
        re.send(1, START, k - 1, k % 2)

    for stage, at_step in ((1, 3), (2, 5), (3, 6), (4, 7)):

        @when(t == at_step, k > 0)
        def _(stage=stage):
            re.turn(stage, k - 1, k % 2)

    @when(t == 1, k > 1)
    def _():
        re.send(5, WAIT, k - 2, (k - 1) % 2)

    @when(i == 1)
    def _():
        for c in range(last):
            bring("first", WAIT, c)
            bring("second", START, c)

    @when(i == 3)
    def _():
        for c in range(last):
            bring("second", WAIT, c)
        bring("third", START, 0)
        bring("down", START, 1)

    @when(i == MINE)
    def _():
        to_a.wait()

    @when(i == 5)
    def _():
        bring("third", START, 1)

    @when(i == TILES - 1)
    def _():
        bring("third", WAIT, 0)
        bring("down", WAIT, 0)

    @when(i == TILES)
    def _():
        bring("third", START, 2)
        bring("down", START, 2)

    @when(i == TILES + 2)
    def _():
        bring("third", WAIT, 1)
        bring("down", WAIT, 1)

    @when(i == 2 * TILES)
    def _():
        bring("third", WAIT, 2)
        bring("down", WAIT, 2)

    @when(t == TILES - 1, k < last)
    def _():
        ga.load(START, (k, (k + 1) % 2), v, wsem)

    @when(k == last, t >= 1, t <= MINE)
    def _():
        part(t - 1 + MINE).start()

    @when(k == last, t > MINE)
    def _():
        keep(t - 1 - MINE).start()

    tile = tile_of(i)
    rows = rows_of(tile)
    s = k % 2
    at = a[rows]
    by = jnp.where(tile < MINE, dy[...], dyp[...])
    mg, mu, md = matrix(vg, s), matrix(vu, s), vd[s].reshape(WIDE, D)
    hidden, dg, du = gradients_of(nn(at, mg), nn(at, mu), nt(by, md).astype(BF).astype(F32))
    fresh = t == 0
    ag[...] = jnp.where(fresh, 0, ag[...]) + tn(at, dg)
    au[...] = jnp.where(fresh, 0, au[...]) + tn(at, du)
    ad[...] = jnp.where(fresh, 0, ad[...]) + tn(hidden, by)
    da[rows] = jnp.where(k == 0, 0, da[rows]) + (nt(dg, mg) + nt(du, mu))

    @when(t == TILES - 1)
    def _():
        re.put(ag, au, ad)

    @when(i == CHUNKS * TILES - 1)
    def _():
        keep(MINE - 1).start()
        outs = [pltpu.make_async_copy(re.w[j], (kg, ku, kd)[j], wsem.at[j]) for j in range(3)]
        for o in outs:
            o.start()
        for j in range(MINE):
            keep(j).wait()
            part(MINE + j).wait()
        for o in outs:
            o.wait()
        re.send(5, WAIT, last - 1, last % 2)


def middle(dy, dyp, n, f4, weights):
    near = pl.BlockSpec((TILE, D), lambda i: (jnp.minimum(tile_of(i), MINE - 1), 0))
    far = pl.BlockSpec((TILE, D), lambda i: (jnp.maximum(tile_of(i) - MINE, 0), 0))
    half = jax.ShapeDtypeStruct((OWN, D), F32)
    raw = jax.ShapeDtypeStruct(SLICED, BF)
    outs = [half, half, *reduced_shapes(SLOTS), raw, raw, jax.ShapeDtypeStruct(BLOCKS, BF)]
    shapes = outs + gathered_shapes(CHUNKS - 1)
    return pl.pallas_call(
        middle_kernel,
        grid=(CHUNKS * TILES,),
        in_specs=[near, far] + [ANY] * (1 + 3 + 3),
        out_specs=[ANY] * len(shapes),
        out_shape=shapes,
        scratch_shapes=[
            pltpu.VMEM((TOKENS, D), BF), pltpu.VMEM((TOKENS, D), F32), *sums(),
            *chunk_buffers(), *gather_scratch(CHUNKS - 1), DMA((3,)), DMA((MINE,)), DMA((2,)), DMA((2, MINE)), *Reduce.scratch(),
        ],
        compiler_params=params(2),
        name="middle",
    )(dy, dyp, n, *f4, *weights)[: len(outs)]


def sums():
    return [pltpu.VMEM((D, WIDE), F32), pltpu.VMEM((D, WIDE), F32), pltpu.VMEM((WIDE, D), F32)]


def back_kernel(g_in, u_in, a_in, down, dao, dar, h, dy, kg, ku, kd, *refs):
    sums_, scratch = refs[3:6], refs[6:]
    b, ag, au, ad, pf, pb, csem, esem, dsem = scratch[:9]
    i = pl.program_id(0)
    k, t = i // TILES, i % TILES
    me = Place()
    re = Reduce(me, scratch[9:], sums_)
    to_b = remote(b.at[block(0, OWN)], b.at[block(1, OWN)], esem.at[0], esem.at[1], me.plus(core=1))
    begun = CHUNKS - 1

    @when(i == 0)
    def _():
        raws = [pltpu.make_async_copy((kg, ku, kd)[j], re.w[j], csem.at[j]) for j in range(3)]
        for o in raws:
            o.start()

        def piece(act, j):
            r, s = block(j, QUARTER), j % 2
            for n, (src, dst) in enumerate(((dao, pf.at[s, 0]), (dar, pf.at[s, 1]), (h, pb.at[s, 0]), (dy, pb.at[s, 1]))):
                act(pltpu.make_async_copy(src.at[r], dst, dsem.at[s, n]))

        piece(START, 0)
        greet(me)
        for o in raws:
            o.wait()
        re.send(1, START, begun, 0)

        def one(j, _):
            @when(j + 1 < OWN // QUARTER)
            def _():
                piece(START, j + 1)

            piece(WAIT, j)
            s = j % 2
            by_a = (pf[s, 0] + pf[s, 1]).astype(BF)
            by_h = jax.vjp(normed, pb[s, 0])[1](by_a)[0]
            b[block(j, QUARTER)] = (pb[s, 1].astype(F32) + by_h.astype(F32)).astype(BF)
            return 0

        lax.fori_loop(0, OWN // QUARTER, one, 0)
        to_b.start()

    @when(i == MINE)
    def _():
        to_b.wait()

    now, before, q = begun + k, begun + k - 1, k % 2

    @when(t == 0, k > 0)
    def _():
        re.send(1, START, now, q)

    @when(t == 1, k > 0)
    def _():
        @when(k > 1)
        def _():
            re.send(5, WAIT, before - 1, q)

        re.turn(3, before, 1 - q)

    @when(t == 5)
    def _():
        re.turn(1, now, q)

        @when(k > 0)
        def _():
            re.turn(4, before, 1 - q)

    @when(t == 7)
    def _():
        re.turn(2, now, q)

    at, by = a_in[...], b[rows_of(tile_of(i))]
    hidden, dg, du = gradients_of(g_in[0], u_in[0], nt(by, down[0].reshape(WIDE, D)).astype(BF).astype(F32))
    fresh = t == 0
    ag[...] = jnp.where(fresh, 0, ag[...]) + tn(at, dg)
    au[...] = jnp.where(fresh, 0, au[...]) + tn(at, du)
    ad[...] = jnp.where(fresh, 0, ad[...]) + tn(hidden, by)

    @when(t == TILES - 1)
    def _():
        re.put(ag, au, ad)

    @when(i == CHUNKS * TILES - 1)
    def _():
        end = SLOTS - 1
        q, p = CHUNKS % 2, 1 - CHUNKS % 2
        re.send(1, START, end, q)
        re.send(5, WAIT, end - 2, q)
        re.turn(3, end - 1, p)
        re.turn(1, end, q)
        re.turn(4, end - 1, p)
        for stage in (2, 3, 4):
            re.turn(stage, end, q)
        re.send(5, WAIT, end - 1, p)
        re.send(5, WAIT, end, q)


def backward(g, u, a, down, half, raw, sums_):
    wide = pl.BlockSpec((1, TILE, WIDE), lambda i: (i // TILES, tile_of(i), 0))
    blocks = [wide, wide, pl.BlockSpec((TILE, D), lambda i: (tile_of(i), 0)), pl.BlockSpec((1,) + BLOCKS, lambda i: (i // TILES, 0, 0, 0))]
    args = (g, u, a, down, *half, *raw, *sums_)
    at = len(args) - len(sums_)
    return pl.pallas_call(
        back_kernel,
        grid=(CHUNKS * TILES,),
        in_specs=blocks + [ANY] * (len(args) - len(blocks)),
        out_specs=[ANY] * len(sums_),
        out_shape=reduced_shapes(SLOTS),
        input_output_aliases={at + i: i for i in range(len(sums_))},
        scratch_shapes=[
            pltpu.VMEM((TOKENS, D), BF), *sums(), pltpu.VMEM((2, 2, QUARTER, D), F32), pltpu.VMEM((2, 2, QUARTER, D), BF),
            DMA((3,)), DMA((2,)), DMA((2, 4)), *Reduce.scratch(),
        ],
        compiler_params=params(3),
        name="backward",
    )(*args)


def adamw(w, m, v, g):
    m = 0.9 * m + 0.1 * g
    v = 0.95 * v + 0.05 * g * g
    step = m * lax.rsqrt(v + 1e-8) + 0.1 * w
    return (w - 0.02 * step).astype(BF), m, v


def update_kernel(gg, gu, gd, *refs):
    ins, outs = refs[:9], refs[9:]
    deep = gd[0]
    sides = [jnp.concatenate([r[k, 0, 0].reshape(LANES, LANES) for k in range(CHUNKS)], axis=1) for r in (gg, gu)]
    for n, g in enumerate((*sides, deep)):
        w, m, v = (r[0] for r in ins[n::3])
        for out, new in zip(outs[n::3], adamw(w.astype(F32), m, v, g.astype(F32))):
            out[0] = new


def update(sums_, arrays):
    half = LANES // 2
    side = pl.BlockSpec((1, LANES, WIDE), lambda i: (i // SLOTS, 0, i % SLOTS))
    deep = pl.BlockSpec((1, half, D), lambda i: (i // SLOTS, i % SLOTS, 0))
    part = pl.BlockSpec((CHUNKS, 1, 1, SIDE, PART, LANES), lambda i: (1 - i // SLOTS, i % 2, i % SLOTS // 2, 0, 0, 0))
    down = pl.BlockSpec((1, half, D), lambda i: ((1 - i // SLOTS) * CHUNKS + i % SLOTS // 2, i % 2, 0))
    return pl.pallas_call(
        update_kernel,
        grid=(2 * SLOTS,),
        in_specs=[part, part, down] + [side, side, deep] * 3,
        out_specs=[side, side, deep] * 3,
        out_shape=[jax.ShapeDtypeStruct(x.shape, x.dtype) for x in arrays],
        compiler_params=pltpu.CompilerParams(vmem_limit_bytes=66_000_000, dimension_semantics=("arbitrary",)),
        name="update",
    )(*sums_, *arrays)


def solution(mesh):
    fine = Mesh(mesh.devices.reshape(SIDE, SIDE, SIDE, 2), AXES)

    def step(x, dy, *arrays):
        x, dy, weights = x[0], dy[0], arrays[:3]
        g0, u0, a0, h1, n1, dyp, *f = forward(x, dy, weights)
        dao, dar, *rest = middle(dy, dyp, n1, f, weights)
        return update(backward(g0, u0, a0, f[2], (dao, dar, h1, dy), rest[3:], rest[:3]), arrays)

    states, cut = P(AXES, None, None), P(None, ("x", "core"), None)
    return jax.shard_map(
        step,
        mesh=fine,
        in_specs=(states, states) + (cut,) * 9,
        out_specs=(cut,) * 9,
        check_vma=False,
    )
```

time: 941 us -> 489 us (0.52)
  Pallas kernels: 0 us -> 487 us
  waiting for transfers between devices: 436 us -> 0 us
  matrix products: 429 us -> 0 us
  other arithmetic: 28.1 us -> 0 us
  local copies, waits for them, and re-layouts: 23.9 us -> 0 us
  between operations: 14.6 us -> 0.82 us
    pallas_call x0 -> x4, Pallas kernels: none -> 487 us  [the longest x1 186 us: middle(): pl.pallas_call(middle_kernel, grid=(CHUNKS * TILES,), in_specs=[near, far...]
    dot_general x15 -> x0, matrix products: 429 us -> none  [the longest x5 156 us: layer(): gate = jnp.dot(a, w['w_gate'], preferred_element_type=jnp.float32)]
    reduce_scatter x6 -> x0, waiting for transfers between devices: 154 us -> none  [summed(): lax.psum_scatter(term, 's', scatter_dimension=0, tiled=True)]
    all_gather x6 -> x0, waiting for transfers between devices: 153 us -> none  [fetched(): lax.all_gather(w[number], 's', axis=0, tiled=True)]
    psum x1 -> x0, waiting for transfers between devices: 127 us -> none  [summed(): lax.psum(lax.psum_scatter(term, 's', scatter_dimension=0, tiled=True), 'r')]
    convert_element_type x2 -> x0, other arithmetic: 21.8 us -> none  [adamw(): return ((w - 0.02 * step).astype(jnp.bfloat16), m, v)]
    unnamed x34 -> x0, local copies, waits for them, and re-layouts: 16.2 us -> none
  transfers between devices with their start and end apart: 13 -> 0, of which waited for: 10 -> 0; matrix products, arithmetic and copies ran while one was open for 35% -> 0% of each run, Pallas kernels for 0% -> 0%
where the time goes in v2:
time: 489 us; the launch traced here: 488 us
  Pallas kernels  487 us (100%)
    pallas_call x1, Pallas kernels, middle(): pl.pallas_call(middle_kernel, grid=(CHUNKS * TILES,), in_specs=[near, far...  186 us
    pallas_call x1, Pallas kernels, backward(): pl.pallas_call(back_kernel, grid=(CHUNKS * TILES,), in_specs=blocks + [AN...  163 us
    pallas_call x1, Pallas kernels, forward(): pl.pallas_call(forward_kernel, grid=(steps,), in_specs=[ANY] * 5, out_spe...  110 us
    pallas_call x1, Pallas kernels, update(): pl.pallas_call(update_kernel, grid=(2 * SLOTS,), in_specs=[part, part, do...  27.4 us

profile of v2, /device:TPU:1, one launch (start us, length us, event | category | flops | bytes accessed | tf_op | source)
XLA Modules:
  0.0 488.3 jit_solution(13462924005531272754)
XLA Ops:
  0.6 110.3 %forward.1 = (f32[4,4096,512]{2,1,0:T(8,128)}, f32[4,4096,512]{2,1,0:T(8,128)}, bf16[4096,1024]{1,0:T(8,128)(2,1)}, bf16[2048,1024]{1,0:T(8,128)(2,1)}, bf16[204...) custom-call(bf16[2048,1024]{1,0:T(8,128)(2,1)} %bitcast.5, ...), custom_call_target="tpu_custom_call" | custom-call | tf_op jit(solution)/shard_map/forward/pallas_call | solution.py:400
  110.9 186.3 %middle.1 = (f32[2048,1024]{1,0:T(8,128)}, f32[2048,1024]{1,0:T(8,128)}, bf16[8,2,4,4,32,128]{5,4,3,2,1,0:T(8,128)(2,1)}, bf16[8,2,4,4,32,128]{5,4,3,2,1,0:T(8,1...) custom-call(bf16[2048,1024]{1,0:T(8,128)(2,1)} %bitcast.3, ...), custom_call_target="tpu_custom_call" | custom-call | tf_op jit(solution)/shard_map/middle/pallas_call | solution.py:565
  297.3 163.4 %backward.1 = (bf16[8,2,4,4,32,128]{5,4,3,2,1,0:T(8,128)(2,1)}, bf16[8,2,4,4,32,128]{5,4,3,2,1,0:T(8,128)(2,1)}, bf16[8,128,1024]{2,1,0:T(8,128)(2,1)}) custom-call(f32[4,4096,512]{2,1,0:T(8,128)} %get-tuple-element.29.g_in, f32[4,4096,512]{2,1,0:T(8,128)} %get-tuple-element.30.u_in, ...), custom_call_target="tpu_custom_call", output_to_operand_aliasing={{0}: (11, {}), {1}: (12, {}), {2}: (13, {})} | custom-call | tf_op jit(solution)/shard_map/backward/pallas_call | solution.py:687
  460.7 27.4 %update.1 = (bf16[2,128,4096]{2,1,0:T(8,128)(2,1)}, bf16[2,128,4096]{2,1,0:T(8,128)(2,1)}, bf16[2,512,1024]{2,1,0:T(8,128)(2,1)}, f32[2,128,4096]{2,1,0:T(8,128)...) custom-call(bf16[8,2,4,4,32,128]{5,4,3,2,1,0:T(8,128)(2,1)} %get-tup, ...), custom_call_target="tpu_custom_call" | custom-call | tf_op jit(solution)/shard_map/update/pallas_call | solution.py:726

commit v3 on v2

--- a/solution.py
+++ b/solution.py
@@ -19,11 +19,13 @@
 TOKENS = 2 * OWN
 CHUNKS = 4
 WIDE = 512
-TILE = 512
+HALVES = [slice(0, WIDE // 2), slice(WIDE // 2, WIDE)]
+TILE = 1024
 TILES = TOKENS // TILE
 MINE = OWN // TILE
 START, WAIT = (lambda c: c.start()), (lambda c: c.wait())
 LANES, PART, QUARTER, SLOTS = 128, 32, 256, 8
+PIECES = OWN // QUARTER
 SLICED = (SIDE, 8, SIDE, PART, LANES)
 BLOCKS = (SIDE, LANES, D)
 
@@ -143,8 +145,7 @@
 
 
 class Reduce:
-    BASE = (0, 9, 18, 35, 44)
-    SEMS = (2, 53)
+    BASE = (0, 9, 18, 35)
 
     @staticmethod
     def scratch():
@@ -158,14 +159,14 @@
             came(8, PART, LANES), came(8, PART, LANES), came(PART, D),
             held(8, PART, LANES), held(8, PART, LANES), held(PART, D),
             v((2, 8, PART, LANES), BF), v((2, 8, PART, LANES), BF), came(PART, QUARTER),
-            held(2, PART, LANES), held(2, PART, LANES), held(PART, QUARTER),
-            DMA(Reduce.SEMS), DMA(Reduce.SEMS), DMA((2, 3)),
+            held(2, 2, PART, LANES), held(2, 2, PART, LANES), held(2, PART, QUARTER),
+            DMA((2, 44)), DMA((2, 44)), DMA((SIDE, 9)), DMA((SIDE, 9)), DMA((2, 3)),
         ]
 
     def __init__(self, me, scratch, out):
         self.me, self.out = me, out
         self.w, self.r1, self.b1, self.r2, self.b2, self.r3, self.b3 = (scratch[3 * i : 3 * i + 3] for i in range(7))
-        self.ss, self.rs, self.ls = scratch[-3:]
+        self.ss, self.rs, self.sl, self.rl, self.ls = scratch[-5:]
 
     def put(self, g, u, d):
         for w, acc in ((self.w[0], g), (self.w[1], u)):
@@ -175,7 +176,7 @@
 
     def copies(self, stage, slot, q):
         me = self.me
-        (g, u, d), row = self.out, block(me.y, PART)
+        (g, u, d), row, col = self.out, block(me.y, PART), block(me.z, QUARTER)
         if stage == 1:
             for n, by in enumerate(OTHERS):
                 y, z, x = (me.along(a, by) for a in ("y", "z", "x"))
@@ -198,25 +199,28 @@
                 yield self.b2[2].at[:, cols], self.r3[2].at[q, n], me.plus(z=by)
         elif stage == 4:
             for by in OTHERS:
-                yield self.b3[0], g.at[slot, :, me.y, me.z], me.plus(z=by)
-                yield self.b3[1], u.at[slot, :, me.y, me.z], me.plus(y=by)
-                yield self.b3[2], d.at[slot, row, block(me.z, QUARTER)], me.plus(z=by)
+                yield self.b3[0].at[q], g.at[slot, :, me.y, me.z], me.plus(z=by)
+                yield self.b3[1].at[q], u.at[slot, :, me.y, me.z], me.plus(y=by)
+                yield self.b3[2].at[q], d.at[slot, row, col], me.plus(y=by)
         else:
             for by in OTHERS:
                 yield g.at[slot, :, me.y], g.at[slot, :, me.y], me.plus(y=by)
                 yield u.at[slot, :, :, me.z], u.at[slot, :, :, me.z], me.plus(z=by)
-                yield d.at[slot, row], d.at[slot, row], me.plus(y=by)
+                yield d.at[slot, :, col], d.at[slot, :, col], me.plus(z=by)
 
     def send(self, stage, act, slot, q):
         me = self.me
         for n, (src, dst, to) in enumerate(self.copies(stage, slot, q)):
-            n += self.BASE[stage - 1]
-            act(remote(src, dst, self.ss.at[q, n], self.rs.at[q, n], to))
+            if stage > SIDE:
+                act(remote(src, dst, self.sl.at[slot % SIDE, n], self.rl.at[slot % SIDE, n], to))
+            else:
+                n += self.BASE[stage - 1]
+                act(remote(src, dst, self.ss.at[q, n], self.rs.at[q, n], to))
         if stage == SIDE:
             g, u, d = self.out
             ends = g.at[slot, :, me.y, me.z], u.at[slot, :, me.y, me.z], d.at[slot, block(me.y, PART), block(me.z, QUARTER)]
             for i, dst in enumerate(ends):
-                act(pltpu.make_async_copy(self.b3[i], dst, self.ls.at[q, i]))
+                act(pltpu.make_async_copy(self.b3[i].at[q], dst, self.ls.at[q, i]))
 
     def add(self, stage, q):
         me = self.me
@@ -228,8 +232,8 @@
                     total = r[q, c].astype(F32)
                     for x in OTHERS:
                         total += r[q, 2 * x + c].astype(F32)
-                    b[c] = total.astype(BF)
-            parts = ((self.b2[2].at[:, cols], self.r3[2], self.b3[2]),)
+                    b[q, c] = total.astype(BF)
+            parts = ((self.b2[2].at[:, cols], self.r3[2], self.b3[2].at[q]),)
         elif stage == 2:
             own = self.b1[0].at[:, me.z], self.b1[1].at[me.y], self.b1[2].at[block(me.y, PART)]
             parts = zip(own, self.r2, self.b2)
@@ -276,7 +280,7 @@
     return pltpu.CompilerParams(collective_id=collective_id, has_side_effects=True, vmem_limit_bytes=66_000_000, dimension_semantics=("arbitrary",))
 
 
-def forward_kernel(x, dy, wg, wu, wd, g_out, u_out, a_out, h_out, n_out, dyp, gf, uf, df, a, xv, acc, prt, vg, vu, vd, ss, rs, ls, wsem, csem, esem, psem):
+def forward_kernel(x, dy, wg, wu, wd, g_out, u_out, a_out, h_out, n_out, dys, gf, uf, df, a, xv, acc, prt, held, vg, vu, vd, ss, rs, ls, wsem, csem, esem, psem, dsem):
     i = pl.program_id(0)
     k, t = i // TILES, i % TILES
     me = Place()
@@ -284,7 +288,14 @@
     v = (vg, vu, vd)
     other = me.plus(core=1)
     mine, theirs = pl.ds(0, OWN), pl.ds(OWN, OWN)
-    to_dy = remote(dy, dyp, esem.at[0], esem.at[1], other)
+    to_dy = remote(dy, dys.at[theirs], esem.at[0], esem.at[1], other)
+
+    def stage(out, j):
+        s = j % 2
+        if out:
+            return pltpu.make_async_copy(held.at[s], dys.at[block(j, QUARTER)], dsem.at[1, s])
+        return pltpu.make_async_copy(dy.at[block(j, QUARTER)], held.at[s], dsem.at[0, s])
+
     to_a = remote(a.at[mine], a.at[theirs], esem.at[2], esem.at[3], other)
     save_a = pltpu.make_async_copy(a, a_out, csem.at[0])
 
@@ -302,9 +313,10 @@
         fetch = pltpu.make_async_copy(x, xv, csem.at[1])
         fetch.start()
         greet(me)
-        for m in range(3):
+        spread(0, START, "first")
+        spread(0, START, "down")
+        for m in range(1, CHUNKS + 1):
             spread(m, START, "first")
-        spread(0, START, "down")
         fetch.wait()
 
         def norm(j, _):
@@ -312,39 +324,57 @@
             a[r] = normed(xv[r])
             return 0
 
-        lax.fori_loop(0, OWN // QUARTER, norm, 0)
+        lax.fori_loop(0, PIECES, norm, 0)
         spread(0, WAIT, "first")
         spread(0, START, "second")
         to_a.start()
         spread(0, WAIT, "second")
         spread(0, START, "third")
-        spread(1, WAIT, "first")
-        spread(1, START, "second")
+        for m in (1, 2):
+            spread(m, WAIT, "first")
+            spread(m, START, "second")
         spread(0, WAIT, "third")
         spread(0, WAIT, "down")
         ga.load(START, (0, 0), v, wsem)
+        spread(1, WAIT, "second")
+        spread(1, START, "third")
 
     @pl.when(t == 0)
     def _():
         ga.load(WAIT, (k, k % 2), v, wsem)
-        spread(k + 1, WAIT, "second")
-        spread(k + 1, START, "third")
         spread(k + 1, START, "down")
 
-        @pl.when(k < 3)
+    @when(t == 1, k < 3)
+    def _():
+        @when(k < 2)
         def _():
-            spread(k + 2, WAIT, "first")
-            spread(k + 2, START, "second")
-
-        @pl.when(k < 2)
-        def _():
-            spread(k + 3, START, "first")
+            spread(k + 3, WAIT, "first")
+            spread(k + 3, START, "second")
+
+        spread(k + 2, WAIT, "second")
+        spread(k + 2, START, "third")
 
     @pl.when(i == MINE)
     def _():
         to_a.wait()
         save_a.start()
         to_dy.start()
+
+    j = i - MINE
+
+    @when(j >= 2, j < PIECES)
+    def _():
+        stage(True, j - 2).wait()
+
+    @when(j >= 0, j < PIECES)
+    def _():
+        stage(False, j).start()
+
+    @when(j >= 1, j <= PIECES)
+    def _():
+        stage(False, j - 1).wait()
+        stage(True, j - 1).start()
+
 
     @when(t == TILES - 1, k < CHUNKS - 1)
     def _():
@@ -373,23 +403,26 @@
         for j in range(MINE):
             part(MINE + j).wait()
 
+        keep = pltpu.make_async_copy(xv, h_out, csem.at[1])
+        keep_n = pltpu.make_async_copy(a.at[mine], n_out, csem.at[2])
+
         def end(j, _):
             r = block(j, QUARTER)
             h = (xv[r].astype(F32) + (acc[r] + prt[r]).astype(BF).astype(F32)).astype(BF)
             xv[r] = h
             a[r] = normed(h)
+            pltpu.make_async_copy(xv.at[r], h_out.at[r], csem.at[1]).start()
+            pltpu.make_async_copy(a.at[r], n_out.at[r], csem.at[2]).start()
             return 0
 
-        lax.fori_loop(0, OWN // QUARTER, end, 0)
-        keep = pltpu.make_async_copy(xv, h_out, csem.at[1])
-        keep2 = pltpu.make_async_copy(a.at[mine], n_out, csem.at[2])
-        keep.start()
-        keep2.start()
+        lax.fori_loop(0, PIECES, end, 0)
         to_dy.wait()
+        for j in (2, 1):
+            stage(True, PIECES - j).wait()
         spread(CHUNKS, WAIT, "third")
         spread(CHUNKS, WAIT, "down")
         keep.wait()
-        keep2.wait()
+        keep_n.wait()
 
 
 def forward(x, dy, weights):
@@ -402,10 +435,10 @@
         grid=(steps,),
         in_specs=[ANY] * 5,
         out_specs=[wide, wide] + [ANY] * 7,
-        out_shape=[big, big, jax.ShapeDtypeStruct((TOKENS, D), BF), own, own, own] + gathered_shapes(CHUNKS + 1),
+        out_shape=[big, big, jax.ShapeDtypeStruct((TOKENS, D), BF), own, own, jax.ShapeDtypeStruct((TOKENS, D), BF)] + gathered_shapes(CHUNKS + 1),
         scratch_shapes=[
-            pltpu.VMEM((TOKENS, D), BF), pltpu.VMEM((OWN, D), BF), pltpu.VMEM((TOKENS, D), F32), pltpu.VMEM((OWN, D), F32),
-            *chunk_buffers(), *gather_scratch(CHUNKS + 1), DMA((3,)), DMA((3,)), DMA((4,)), DMA((2, MINE)),
+            pltpu.VMEM((TOKENS, D), BF), pltpu.VMEM((OWN, D), BF), pltpu.VMEM((TOKENS, D), F32), pltpu.VMEM((OWN, D), F32), pltpu.VMEM((2, QUARTER, D), BF),
+            *chunk_buffers(), *gather_scratch(CHUNKS + 1), DMA((3,)), DMA((3,)), DMA((4,)), DMA((2, MINE)), DMA((2, 2)),
         ],
         compiler_params=params(1),
         name="forward",
@@ -418,7 +451,7 @@
     return (si * u).astype(BF), (dh * u * (s + si * (1 - s))).astype(BF), (dh * si).astype(BF)
 
 
-def middle_kernel(dy, dyp, n, g4, u4, d4, wg, wu, wd, dao, dar, rg, ru, rd, kg, ku, kd, gf, uf, df, *scratch):
+def middle_kernel(dy, n, g4, u4, d4, wg, wu, wd, dao, dar, rg, ru, rd, kg, ku, kd, gf, uf, df, *scratch):
     a, da, ag, au, ad, vg, vu, vd, ss, rs, ls, wsem, csem, esem, psem, *rest = scratch
     i = pl.program_id(0)
     k, t = i // TILES, i % TILES
@@ -456,63 +489,69 @@
         fetch.wait()
         load(WAIT, (g4, u4, d4), (CHUNKS, 0), v, wsem)
 
+    now, before, q = k - 1, k - 2, k % 2
+
     @when(t == 0, k > 0)
     def _():
         ga.load(WAIT, (k - 1, k % 2), v, wsem)
-        re.send(1, START, k - 1, k % 2)
-
-    for stage, at_step in ((1, 3), (2, 5), (3, 6), (4, 7)):
-
-        @when(t == at_step, k > 0)
+
+        @when(k > 1)
+        def _():
+            re.turn(3, before, 1 - q)
+
+        re.send(1, START, now, q)
+
+    @when(t == 1, k > 1)
+    def _():
+        re.turn(4, before, 1 - q)
+
+    for stage in (1, 2):
+
+        @when(t == stage + 1, k > 0)
         def _(stage=stage):
-            re.turn(stage, k - 1, k % 2)
-
-    @when(t == 1, k > 1)
-    def _():
-        re.send(5, WAIT, k - 2, (k - 1) % 2)
+            re.turn(stage, now, q)
+
+    @when(t == 3, k > 1)
+    def _():
+        re.send(5, WAIT, before, 1 - q)
 
     @when(i == 1)
     def _():
         for c in range(last):
             bring("first", WAIT, c)
+        bring("second", START, 0)
+
+    @when(i == MINE)
+    def _():
+        to_a.wait()
+        bring("second", WAIT, 0)
+        bring("third", START, 0)
+        for c in range(1, last):
             bring("second", START, c)
-
-    @when(i == 3)
-    def _():
-        for c in range(last):
-            bring("second", WAIT, c)
-        bring("third", START, 0)
         bring("down", START, 1)
 
-    @when(i == MINE)
-    def _():
-        to_a.wait()
-
-    @when(i == 5)
-    def _():
+    @when(i == TILES)
+    def _():
+        bring("second", WAIT, 1)
         bring("third", START, 1)
 
-    @when(i == TILES - 1)
-    def _():
-        bring("third", WAIT, 0)
-        bring("down", WAIT, 0)
-
-    @when(i == TILES)
-    def _():
+    @when(i == TILES + 1)
+    def _():
+        bring("down", WAIT, 1)
+        bring("down", START, 2)
+
+    @when(i == TILES + 3)
+    def _():
+        bring("third", WAIT, 1)
+        bring("second", WAIT, 2)
         bring("third", START, 2)
-        bring("down", START, 2)
-
-    @when(i == TILES + 2)
-    def _():
-        bring("third", WAIT, 1)
-        bring("down", WAIT, 1)
-
-    @when(i == 2 * TILES)
+
+    @when(i == 2 * TILES + 1)
     def _():
         bring("third", WAIT, 2)
         bring("down", WAIT, 2)
 
-    @when(t == TILES - 1, k < last)
+    @when(t == TILES - 1, k > 0, k < last)
     def _():
         ga.load(START, (k, (k + 1) % 2), v, wsem)
 
@@ -528,21 +567,26 @@
     rows = rows_of(tile)
     s = k % 2
     at = a[rows]
-    by = jnp.where(tile < MINE, dy[...], dyp[...])
+    by = dy[...]
     mg, mu, md = matrix(vg, s), matrix(vu, s), vd[s].reshape(WIDE, D)
-    hidden, dg, du = gradients_of(nn(at, mg), nn(at, mu), nt(by, md).astype(BF).astype(F32))
-    fresh = t == 0
-    ag[...] = jnp.where(fresh, 0, ag[...]) + tn(at, dg)
-    au[...] = jnp.where(fresh, 0, au[...]) + tn(at, du)
-    ad[...] = jnp.where(fresh, 0, ad[...]) + tn(hidden, by)
+    parts = [gradients_of(nn(at, mg[:, c]), nn(at, mu[:, c]), nt(by, md[c]).astype(BF).astype(F32)) for c in HALVES]
+    sum_up(t == 0, (ag, au, ad), at, by, parts)
+    dg, du = (jnp.concatenate([p[j] for p in parts], axis=1) for j in (1, 2))
     da[rows] = jnp.where(k == 0, 0, da[rows]) + (nt(dg, mg) + nt(du, mu))
 
+    @when(i == TILES - 1)
+    def _():
+        bring("third", WAIT, 0)
+        bring("down", WAIT, 0)
+        ga.load(START, (0, 1), v, wsem)
+
     @when(t == TILES - 1)
     def _():
         re.put(ag, au, ad)
 
     @when(i == CHUNKS * TILES - 1)
     def _():
+        re.turn(3, last - 1, last % 2)
         keep(MINE - 1).start()
         outs = [pltpu.make_async_copy(re.w[j], (kg, ku, kd)[j], wsem.at[j]) for j in range(3)]
         for o in outs:
@@ -552,12 +596,10 @@
             part(MINE + j).wait()
         for o in outs:
             o.wait()
-        re.send(5, WAIT, last - 1, last % 2)
-
-
-def middle(dy, dyp, n, f4, weights):
-    near = pl.BlockSpec((TILE, D), lambda i: (jnp.minimum(tile_of(i), MINE - 1), 0))
-    far = pl.BlockSpec((TILE, D), lambda i: (jnp.maximum(tile_of(i) - MINE, 0), 0))
+        re.send(4, WAIT, last - 1, last % 2)
+
+
+def middle(dy, n, f4, weights):
     half = jax.ShapeDtypeStruct((OWN, D), F32)
     raw = jax.ShapeDtypeStruct(SLICED, BF)
     outs = [half, half, *reduced_shapes(SLOTS), raw, raw, jax.ShapeDtypeStruct(BLOCKS, BF)]
@@ -565,7 +607,7 @@
     return pl.pallas_call(
         middle_kernel,
         grid=(CHUNKS * TILES,),
-        in_specs=[near, far] + [ANY] * (1 + 3 + 3),
+        in_specs=[pl.BlockSpec((TILE, D), lambda i: (tile_of(i), 0))] + [ANY] * (1 + 3 + 3),
         out_specs=[ANY] * len(shapes),
         out_shape=shapes,
         scratch_shapes=[
@@ -574,7 +616,15 @@
         ],
         compiler_params=params(2),
         name="middle",
-    )(dy, dyp, n, *f4, *weights)[: len(outs)]
+    )(dy, n, *f4, *weights)[: len(outs)]
+
+
+def sum_up(fresh, sums_, at, by, parts):
+    ag, au, ad = sums_
+    for c, (hidden, dg, du) in zip(HALVES, parts):
+        ag[:, c] = jnp.where(fresh, 0, ag[:, c]) + tn(at, dg)
+        au[:, c] = jnp.where(fresh, 0, au[:, c]) + tn(at, du)
+        ad[c] = jnp.where(fresh, 0, ad[c]) + tn(hidden, by)
 
 
 def sums():
@@ -606,10 +656,11 @@
         greet(me)
         for o in raws:
             o.wait()
+        re.send(5, START, begun - 1, 1)
         re.send(1, START, begun, 0)
 
         def one(j, _):
-            @when(j + 1 < OWN // QUARTER)
+            @when(j + 1 < PIECES)
             def _():
                 piece(START, j + 1)
 
@@ -620,7 +671,7 @@
             b[block(j, QUARTER)] = (pb[s, 1].astype(F32) + by_h.astype(F32)).astype(BF)
             return 0
 
-        lax.fori_loop(0, OWN // QUARTER, one, 0)
+        lax.fori_loop(0, PIECES, one, 0)
         to_b.start()
 
     @when(i == MINE)
@@ -635,30 +686,32 @@
 
     @when(t == 1, k > 0)
     def _():
+        re.turn(2, before, 1 - q)
+
+        @when(k == 3)
+        def _():
+            re.send(5, WAIT, before - 2, 1 - q)
+
         @when(k > 1)
         def _():
+            re.turn(4, before - 1, q)
+
+    @when(t == 3)
+    def _():
+        @when(k == 1)
+        def _():
             re.send(5, WAIT, before - 1, q)
 
-        re.turn(3, before, 1 - q)
-
-    @when(t == 5)
-    def _():
         re.turn(1, now, q)
 
         @when(k > 0)
         def _():
-            re.turn(4, before, 1 - q)
-
-    @when(t == 7)
-    def _():
-        re.turn(2, now, q)
+            re.turn(3, before, 1 - q)
 
     at, by = a_in[...], b[rows_of(tile_of(i))]
-    hidden, dg, du = gradients_of(g_in[0], u_in[0], nt(by, down[0].reshape(WIDE, D)).astype(BF).astype(F32))
-    fresh = t == 0
-    ag[...] = jnp.where(fresh, 0, ag[...]) + tn(at, dg)
-    au[...] = jnp.where(fresh, 0, au[...]) + tn(at, du)
-    ad[...] = jnp.where(fresh, 0, ad[...]) + tn(hidden, by)
+    md = down[0].reshape(WIDE, D)
+    parts = [gradients_of(g_in[0, :, c], u_in[0, :, c], nt(by, md[c]).astype(BF).astype(F32)) for c in HALVES]
+    sum_up(t == 0, (ag, au, ad), at, by, parts)
 
     @when(t == TILES - 1)
     def _():
@@ -669,12 +722,16 @@
         end = SLOTS - 1
         q, p = CHUNKS % 2, 1 - CHUNKS % 2
         re.send(1, START, end, q)
+        re.send(5, WAIT, end - 3, p)
+        re.turn(4, end - 2, q)
+        re.turn(2, end - 1, p)
+        re.turn(1, end, q)
+        re.turn(3, end - 1, p)
+        re.turn(2, end, q)
+        re.turn(3, end, q)
+        re.turn(4, end - 1, p)
         re.send(5, WAIT, end - 2, q)
-        re.turn(3, end - 1, p)
-        re.turn(1, end, q)
-        re.turn(4, end - 1, p)
-        for stage in (2, 3, 4):
-            re.turn(stage, end, q)
+        re.turn(4, end, q)
         re.send(5, WAIT, end - 1, p)
         re.send(5, WAIT, end, q)
 
@@ -709,23 +766,21 @@
 
 def update_kernel(gg, gu, gd, *refs):
     ins, outs = refs[:9], refs[9:]
-    deep = gd[0]
-    sides = [jnp.concatenate([r[k, 0, 0].reshape(LANES, LANES) for k in range(CHUNKS)], axis=1) for r in (gg, gu)]
-    for n, g in enumerate((*sides, deep)):
+    sides = [jnp.concatenate([r[k, c, 0].reshape(LANES, LANES) for c in range(2) for k in range(CHUNKS)], axis=1) for r in (gg, gu)]
+    for n, g in enumerate((*sides, gd[0])):
         w, m, v = (r[0] for r in ins[n::3])
         for out, new in zip(outs[n::3], adamw(w.astype(F32), m, v, g.astype(F32))):
             out[0] = new
 
 
 def update(sums_, arrays):
-    half = LANES // 2
-    side = pl.BlockSpec((1, LANES, WIDE), lambda i: (i // SLOTS, 0, i % SLOTS))
-    deep = pl.BlockSpec((1, half, D), lambda i: (i // SLOTS, i % SLOTS, 0))
-    part = pl.BlockSpec((CHUNKS, 1, 1, SIDE, PART, LANES), lambda i: (1 - i // SLOTS, i % 2, i % SLOTS // 2, 0, 0, 0))
-    down = pl.BlockSpec((1, half, D), lambda i: ((1 - i // SLOTS) * CHUNKS + i % SLOTS // 2, i % 2, 0))
+    side = pl.BlockSpec((1, LANES, D), lambda i: (i // SIDE, 0, i % SIDE))
+    deep = pl.BlockSpec((1, LANES, D), lambda i: (i // SIDE, i % SIDE, 0))
+    part = pl.BlockSpec((CHUNKS, 2, 1, SIDE, PART, LANES), lambda i: (1 - i // SIDE, 0, i % SIDE, 0, 0, 0))
+    down = pl.BlockSpec((1, LANES, D), lambda i: ((1 - i // SIDE) * CHUNKS + i % SIDE, 0, 0))
     return pl.pallas_call(
         update_kernel,
-        grid=(2 * SLOTS,),
+        grid=(SLOTS,),
         in_specs=[part, part, down] + [side, side, deep] * 3,
         out_specs=[side, side, deep] * 3,
         out_shape=[jax.ShapeDtypeStruct(x.shape, x.dtype) for x in arrays],
@@ -739,8 +794,8 @@
 
     def step(x, dy, *arrays):
         x, dy, weights = x[0], dy[0], arrays[:3]
-        g0, u0, a0, h1, n1, dyp, *f = forward(x, dy, weights)
-        dao, dar, *rest = middle(dy, dyp, n1, f, weights)
+        g0, u0, a0, h1, n1, dys, *f = forward(x, dy, weights)
+        dao, dar, *rest = middle(dys, n1, f, weights)
         return update(backward(g0, u0, a0, f[2], (dao, dar, h1, dy), rest[3:], rest[:3]), arrays)
 
     states, cut = P(AXES, None, None), P(None, ("x", "core"), None)

time: 489 us -> 456 us (0.933)
  Pallas kernels: 487 us -> 455 us
    pallas_call x2, Pallas kernels: 214 us -> 194 us  [the longest x1 170 us: middle(): pl.pallas_call(middle_kernel, grid=(CHUNKS * TILES,), in_specs=[pl.BlockS...]
    pallas_call x1, Pallas kernels: 163 us -> 149 us  [backward(): pl.pallas_call(back_kernel, grid=(CHUNKS * TILES,), in_specs=blocks + [AN...]
where the time goes in v3:
time: 456 us
  Pallas kernels  455 us (100%)
    pallas_call x1, Pallas kernels, middle(): pl.pallas_call(middle_kernel, grid=(CHUNKS * TILES,), in_specs=[pl.BlockS...  170 us
    pallas_call x1, Pallas kernels, backward(): pl.pallas_call(back_kernel, grid=(CHUNKS * TILES,), in_specs=blocks + [AN...  149 us
    pallas_call x1, Pallas kernels, forward(): pl.pallas_call(forward_kernel, grid=(steps,), in_specs=[ANY] * 5, out_spe...  112 us
    pallas_call x1, Pallas kernels, update(): pl.pallas_call(update_kernel, grid=(SLOTS,), in_specs=[part, part, down]...  24.4 us

profile of v3, /device:TPU:1, one launch (start us, length us, event | category | flops | bytes accessed | tf_op | source)
XLA Modules:
  0.0 456.0 jit_solution(11976645229805139909)
XLA Ops:
  0.6 112.2 %forward.1 = (f32[4,4096,512]{2,1,0:T(8,128)}, f32[4,4096,512]{2,1,0:T(8,128)}, bf16[4096,1024]{1,0:T(8,128)(2,1)}, bf16[2048,1024]{1,0:T(8,128)(2,1)}, bf16[204...) custom-call(bf16[2048,1024]{1,0:T(8,128)(2,1)} %bitcast.4, ...), custom_call_target="tpu_custom_call" | custom-call | tf_op jit(solution)/shard_map/forward/pallas_call | solution.py:433
  112.8 169.6 %middle.1 = (f32[2048,1024]{1,0:T(8,128)}, f32[2048,1024]{1,0:T(8,128)}, bf16[8,2,4,4,32,128]{5,4,3,2,1,0:T(8,128)(2,1)}, bf16[8,2,4,4,32,128]{5,4,3,2,1,0:T(8,1...) custom-call(bf16[4096,1024]{1,0:T(8,128)(2,1)} %get-tuple-element.33, ...), custom_call_target="tpu_custom_call" | custom-call | tf_op jit(solution)/shard_map/middle/pallas_call | solution.py:607
  282.4 149.0 %backward.1 = (bf16[8,2,4,4,32,128]{5,4,3,2,1,0:T(8,128)(2,1)}, bf16[8,2,4,4,32,128]{5,4,3,2,1,0:T(8,128)(2,1)}, bf16[8,128,1024]{2,1,0:T(8,128)(2,1)}) custom-call(f32[4,4096,512]{2,1,0:T(8,128)} %get-tuple-element.29.g_in, f32[4,4096,512]{2,1,0:T(8,128)} %get-tuple-element.30.u_in, ...), custom_call_target="tpu_custom_call", output_to_operand_aliasing={{0}: (11, {}), {1}: (12, {}), {2}: (13, {})} | custom-call | tf_op jit(solution)/shard_map/backward/pallas_call | solution.py:744
  431.4 24.4 %update.1 = (bf16[2,128,4096]{2,1,0:T(8,128)(2,1)}, bf16[2,128,4096]{2,1,0:T(8,128)(2,1)}, bf16[2,512,1024]{2,1,0:T(8,128)(2,1)}, f32[2,128,4096]{2,1,0:T(8,128)...) custom-call(bf16[8,2,4,4,32,128]{5,4,3,2,1,0:T(8,128)(2,1)} %get-tup, ...), custom_call_target="tpu_custom_call" | custom-call | tf_op jit(solution)/shard_map/update/pallas_call | solution.py:781

commit v4 on v3

--- a/solution.py
+++ b/solution.py
@@ -86,6 +86,10 @@
 
 def remote(src, dst, ss, rs, to):
     return pltpu.make_async_remote_copy(src_ref=src, dst_ref=dst, send_sem=ss, recv_sem=rs, device_id=to, device_id_type=MESH)
+
+
+def pair(sems, *at):
+    return sems.at[(0, *at)], sems.at[(1, *at)]
 
 
 class Gather:
@@ -277,7 +281,7 @@
 
 
 def params(collective_id):
-    return pltpu.CompilerParams(collective_id=collective_id, has_side_effects=True, vmem_limit_bytes=66_000_000, dimension_semantics=("arbitrary",))
+    return pltpu.CompilerParams(collective_id=collective_id, has_side_effects=True, vmem_limit_bytes=67_000_000, dimension_semantics=("arbitrary",))
 
 
 def forward_kernel(x, dy, wg, wu, wd, g_out, u_out, a_out, h_out, n_out, dys, gf, uf, df, a, xv, acc, prt, held, vg, vu, vd, ss, rs, ls, wsem, csem, esem, psem, dsem):
@@ -286,9 +290,11 @@
     me = Place()
     ga = Gather(me, (wg, wu, wd), (gf, uf, df), (ss, rs, ls))
     v = (vg, vu, vd)
+    early = Gather(me, (wg, wu, wd), v, (ss, rs, ls))
+    save_d = pltpu.make_async_copy(vd.at[0], df.at[0], csem.at[3])
     other = me.plus(core=1)
-    mine, theirs = pl.ds(0, OWN), pl.ds(OWN, OWN)
-    to_dy = remote(dy, dys.at[theirs], esem.at[0], esem.at[1], other)
+    mine, theirs = block(0, OWN), block(1, OWN)
+    to_dy = remote(dy, dys.at[theirs], *pair(esem, 0), other)
 
     def stage(out, j):
         s = j % 2
@@ -296,17 +302,18 @@
             return pltpu.make_async_copy(held.at[s], dys.at[block(j, QUARTER)], dsem.at[1, s])
         return pltpu.make_async_copy(dy.at[block(j, QUARTER)], held.at[s], dsem.at[0, s])
 
-    to_a = remote(a.at[mine], a.at[theirs], esem.at[2], esem.at[3], other)
+    to_a = remote(a.at[mine], a.at[theirs], *pair(esem, 1), other)
     save_a = pltpu.make_async_copy(a, a_out, csem.at[0])
 
     def spread(m, act, stage):
+        to = getattr(early if isinstance(m, int) and m == 0 else ga, stage)
         if stage in ("first", "down"):
-            getattr(ga, stage)(act, m // CHUNKS, m % CHUNKS, m, m)
+            to(act, m // CHUNKS, m % CHUNKS, m, m)
         else:
-            getattr(ga, stage)(act, m, m)
+            to(act, m, m)
 
     def part(tile):
-        return remote(acc.at[rows_of(tile)], prt.at[rows_of(tile - MINE)], psem.at[0, tile - MINE], psem.at[1, tile - MINE], other)
+        return remote(acc.at[rows_of(tile)], prt.at[rows_of(tile - MINE)], *pair(psem, tile - MINE), other)
 
     @pl.when(i == 0)
     def _():
@@ -314,9 +321,11 @@
         fetch.start()
         greet(me)
         spread(0, START, "first")
+        spread(1, START, "first")
         spread(0, START, "down")
-        for m in range(1, CHUNKS + 1):
+        for m in range(2, CHUNKS + 1):
             spread(m, START, "first")
+        spread(1, START, "down")
         fetch.wait()
 
         def norm(j, _):
@@ -328,21 +337,31 @@
         spread(0, WAIT, "first")
         spread(0, START, "second")
         to_a.start()
+        spread(1, WAIT, "first")
+        spread(1, START, "second")
         spread(0, WAIT, "second")
         spread(0, START, "third")
-        for m in (1, 2):
-            spread(m, WAIT, "first")
-            spread(m, START, "second")
+        spread(2, WAIT, "first")
+        spread(2, START, "second")
         spread(0, WAIT, "third")
         spread(0, WAIT, "down")
-        ga.load(START, (0, 0), v, wsem)
+        save_d.start()
         spread(1, WAIT, "second")
         spread(1, START, "third")
 
-    @pl.when(t == 0)
-    def _():
-        ga.load(WAIT, (k, k % 2), v, wsem)
-        spread(k + 1, START, "down")
+    @when(t == 0)
+    def _():
+        @when(k < CHUNKS - 1)
+        def _():
+            spread(k + 2, START, "down")
+
+        @when(k > 0)
+        def _():
+            ga.load(WAIT, (k, k % 2), v, wsem)
+
+        @when(k == 1)
+        def _():
+            save_d.wait()
 
     @when(t == 1, k < 3)
     def _():
@@ -438,7 +457,7 @@
         out_shape=[big, big, jax.ShapeDtypeStruct((TOKENS, D), BF), own, own, jax.ShapeDtypeStruct((TOKENS, D), BF)] + gathered_shapes(CHUNKS + 1),
         scratch_shapes=[
             pltpu.VMEM((TOKENS, D), BF), pltpu.VMEM((OWN, D), BF), pltpu.VMEM((TOKENS, D), F32), pltpu.VMEM((OWN, D), F32), pltpu.VMEM((2, QUARTER, D), BF),
-            *chunk_buffers(), *gather_scratch(CHUNKS + 1), DMA((3,)), DMA((3,)), DMA((4,)), DMA((2, MINE)), DMA((2, 2)),
+            *chunk_buffers(), *gather_scratch(CHUNKS + 1), DMA((3,)), DMA((4,)), DMA((2, 2)), DMA((2, MINE)), DMA((2, 2)),
         ],
         compiler_params=params(1),
         name="forward",
@@ -451,8 +470,8 @@
     return (si * u).astype(BF), (dh * u * (s + si * (1 - s))).astype(BF), (dh * si).astype(BF)
 
 
-def middle_kernel(dy, n, g4, u4, d4, wg, wu, wd, dao, dar, rg, ru, rd, kg, ku, kd, gf, uf, df, *scratch):
-    a, da, ag, au, ad, vg, vu, vd, ss, rs, ls, wsem, csem, esem, psem, *rest = scratch
+def middle_kernel(dy, dys, h, n, g4, u4, d4, wg, wu, wd, dh, dar, rg, ru, rd, kg, ku, kd, gf, uf, df, *scratch):
+    a, da, ag, au, ad, vg, vu, vd, ss, rs, ls, wsem, csem, esem, psem, dsem, *rest = scratch
     i = pl.program_id(0)
     k, t = i // TILES, i % TILES
     me = Place()
@@ -461,14 +480,11 @@
     v = (vg, vu, vd)
     other = me.plus(core=1)
     mine, theirs = block(0, OWN), block(1, OWN)
-    to_a = remote(n, a.at[theirs], esem.at[0], esem.at[1], other)
+    to_a = remote(n, a.at[theirs], *pair(esem, 0), other)
     last = CHUNKS - 1
 
     def part(tile):
-        return remote(da.at[rows_of(tile)], dar.at[rows_of(tile - MINE)], psem.at[0, tile - MINE], psem.at[1, tile - MINE], other)
-
-    def keep(tile):
-        return pltpu.make_async_copy(da.at[rows_of(tile)], dao.at[rows_of(tile)], csem.at[tile])
+        return remote(da.at[rows_of(tile)], dar.at[rows_of(tile - MINE)], *pair(psem, tile - MINE), other)
 
     def bring(stage, act, c):
         if stage in ("first", "down"):
@@ -519,34 +535,31 @@
     def _():
         for c in range(last):
             bring("first", WAIT, c)
-        bring("second", START, 0)
+            bring("second", START, c)
 
     @when(i == MINE)
     def _():
         to_a.wait()
-        bring("second", WAIT, 0)
+        for c in range(last):
+            bring("second", WAIT, c)
         bring("third", START, 0)
-        for c in range(1, last):
-            bring("second", START, c)
         bring("down", START, 1)
 
-    @when(i == TILES)
-    def _():
-        bring("second", WAIT, 1)
+    @when(i == TILES - 1)
+    def _():
         bring("third", START, 1)
 
     @when(i == TILES + 1)
     def _():
+        bring("third", WAIT, 1)
         bring("down", WAIT, 1)
         bring("down", START, 2)
 
-    @when(i == TILES + 3)
-    def _():
-        bring("third", WAIT, 1)
-        bring("second", WAIT, 2)
+    @when(i == 2 * TILES - 1)
+    def _():
         bring("third", START, 2)
 
-    @when(i == 2 * TILES + 1)
+    @when(i == 2 * TILES + 2)
     def _():
         bring("third", WAIT, 2)
         bring("down", WAIT, 2)
@@ -558,10 +571,6 @@
     @when(k == last, t >= 1, t <= MINE)
     def _():
         part(t - 1 + MINE).start()
-
-    @when(k == last, t > MINE)
-    def _():
-        keep(t - 1 - MINE).start()
 
     tile = tile_of(i)
     rows = rows_of(tile)
@@ -587,36 +596,58 @@
     @when(i == CHUNKS * TILES - 1)
     def _():
         re.turn(3, last - 1, last % 2)
-        keep(MINE - 1).start()
         outs = [pltpu.make_async_copy(re.w[j], (kg, ku, kd)[j], wsem.at[j]) for j in range(3)]
         for o in outs:
             o.start()
         for j in range(MINE):
-            keep(j).wait()
             part(MINE + j).wait()
+
+        def piece(act, j):
+            r, s = block(j, LANES), j % SIDE
+            for n, (src, dst) in enumerate(((dar, ad.at[block(s, LANES)]), (h, vd.at[0, s]), (dys, vd.at[1, s]))):
+                act(pltpu.make_async_copy(src.at[r], dst, dsem.at[s, n]))
+
+        count = OWN // LANES
+        for j in range(SIDE - 1):
+            piece(START, j)
+
+        def one(j, _):
+            @when(j + SIDE - 1 < count)
+            def _():
+                piece(START, j + SIDE - 1)
+
+            piece(WAIT, j)
+            r, s = block(j, LANES), j % SIDE
+            by_h = jax.vjp(normed, vd[0, s])[1]((da[r] + ad[block(s, LANES)]).astype(BF))[0]
+            a[r] = (vd[1, s].astype(F32) + by_h.astype(F32)).astype(BF)
+            pltpu.make_async_copy(a.at[r], dh.at[r], csem.at[0]).start()
+            return 0
+
+        lax.fori_loop(0, count, one, 0)
         for o in outs:
             o.wait()
-        re.send(4, WAIT, last - 1, last % 2)
-
-
-def middle(dy, n, f4, weights):
-    half = jax.ShapeDtypeStruct((OWN, D), F32)
+        re.send(SIDE, WAIT, last - 1, last % 2)
+        pltpu.make_async_copy(a.at[mine], dh, csem.at[0]).wait()
+
+
+def middle(dy, h, n, f4, weights):
     raw = jax.ShapeDtypeStruct(SLICED, BF)
-    outs = [half, half, *reduced_shapes(SLOTS), raw, raw, jax.ShapeDtypeStruct(BLOCKS, BF)]
+    outs = [jax.ShapeDtypeStruct((OWN, D), BF), jax.ShapeDtypeStruct((OWN, D), F32), *reduced_shapes(SLOTS), raw, raw, jax.ShapeDtypeStruct(BLOCKS, BF)]
     shapes = outs + gathered_shapes(CHUNKS - 1)
     return pl.pallas_call(
         middle_kernel,
         grid=(CHUNKS * TILES,),
-        in_specs=[pl.BlockSpec((TILE, D), lambda i: (tile_of(i), 0))] + [ANY] * (1 + 3 + 3),
+        in_specs=[pl.BlockSpec((TILE, D), lambda i: (tile_of(i), 0))] + [ANY] * 9,
         out_specs=[ANY] * len(shapes),
         out_shape=shapes,
         scratch_shapes=[
             pltpu.VMEM((TOKENS, D), BF), pltpu.VMEM((TOKENS, D), F32), *sums(),
-            *chunk_buffers(), *gather_scratch(CHUNKS - 1), DMA((3,)), DMA((MINE,)), DMA((2,)), DMA((2, MINE)), *Reduce.scratch(),
+            *chunk_buffers(), *gather_scratch(CHUNKS - 1), DMA((3,)), DMA((1,)), DMA((2, 1)), DMA((2, MINE)),
+            DMA((SIDE, 3)), *Reduce.scratch(),
         ],
         compiler_params=params(2),
         name="middle",
-    )(dy, n, *f4, *weights)[: len(outs)]
+    )(dy, dy, h, n, *f4, *weights)[: len(outs)]
 
 
 def sum_up(fresh, sums_, at, by, parts):
@@ -631,48 +662,28 @@
     return [pltpu.VMEM((D, WIDE), F32), pltpu.VMEM((D, WIDE), F32), pltpu.VMEM((WIDE, D), F32)]
 
 
-def back_kernel(g_in, u_in, a_in, down, dao, dar, h, dy, kg, ku, kd, *refs):
+def back_kernel(g_in, u_in, a_in, down, dh, kg, ku, kd, *refs):
     sums_, scratch = refs[3:6], refs[6:]
-    b, ag, au, ad, pf, pb, csem, esem, dsem = scratch[:9]
+    b, ag, au, ad, csem, esem, *scratch = scratch
     i = pl.program_id(0)
     k, t = i // TILES, i % TILES
     me = Place()
-    re = Reduce(me, scratch[9:], sums_)
-    to_b = remote(b.at[block(0, OWN)], b.at[block(1, OWN)], esem.at[0], esem.at[1], me.plus(core=1))
+    re = Reduce(me, scratch, sums_)
+    to_b = remote(dh, b.at[block(1, OWN)], *pair(esem, 0), me.plus(core=1))
     begun = CHUNKS - 1
 
     @when(i == 0)
     def _():
         raws = [pltpu.make_async_copy((kg, ku, kd)[j], re.w[j], csem.at[j]) for j in range(3)]
+        raws.append(pltpu.make_async_copy(dh, b.at[block(0, OWN)], csem.at[3]))
         for o in raws:
             o.start()
-
-        def piece(act, j):
-            r, s = block(j, QUARTER), j % 2
-            for n, (src, dst) in enumerate(((dao, pf.at[s, 0]), (dar, pf.at[s, 1]), (h, pb.at[s, 0]), (dy, pb.at[s, 1]))):
-                act(pltpu.make_async_copy(src.at[r], dst, dsem.at[s, n]))
-
-        piece(START, 0)
         greet(me)
+        to_b.start()
         for o in raws:
             o.wait()
+        re.send(1, START, begun, 0)
         re.send(5, START, begun - 1, 1)
-        re.send(1, START, begun, 0)
-
-        def one(j, _):
-            @when(j + 1 < PIECES)
-            def _():
-                piece(START, j + 1)
-
-            piece(WAIT, j)
-            s = j % 2
-            by_a = (pf[s, 0] + pf[s, 1]).astype(BF)
-            by_h = jax.vjp(normed, pb[s, 0])[1](by_a)[0]
-            b[block(j, QUARTER)] = (pb[s, 1].astype(F32) + by_h.astype(F32)).astype(BF)
-            return 0
-
-        lax.fori_loop(0, PIECES, one, 0)
-        to_b.start()
 
     @when(i == MINE)
     def _():
@@ -728,18 +739,18 @@
         re.turn(1, end, q)
         re.turn(3, end - 1, p)
         re.turn(2, end, q)
-        re.turn(3, end, q)
         re.turn(4, end - 1, p)
         re.send(5, WAIT, end - 2, q)
+        re.turn(3, end, q)
         re.turn(4, end, q)
         re.send(5, WAIT, end - 1, p)
         re.send(5, WAIT, end, q)
 
 
-def backward(g, u, a, down, half, raw, sums_):
+def backward(g, u, a, down, dh, raw, sums_):
     wide = pl.BlockSpec((1, TILE, WIDE), lambda i: (i // TILES, tile_of(i), 0))
     blocks = [wide, wide, pl.BlockSpec((TILE, D), lambda i: (tile_of(i), 0)), pl.BlockSpec((1,) + BLOCKS, lambda i: (i // TILES, 0, 0, 0))]
-    args = (g, u, a, down, *half, *raw, *sums_)
+    args = (g, u, a, down, dh, *raw, *sums_)
     at = len(args) - len(sums_)
     return pl.pallas_call(
         back_kernel,
@@ -749,8 +760,7 @@
         out_shape=reduced_shapes(SLOTS),
         input_output_aliases={at + i: i for i in range(len(sums_))},
         scratch_shapes=[
-            pltpu.VMEM((TOKENS, D), BF), *sums(), pltpu.VMEM((2, 2, QUARTER, D), F32), pltpu.VMEM((2, 2, QUARTER, D), BF),
-            DMA((3,)), DMA((2,)), DMA((2, 4)), *Reduce.scratch(),
+            pltpu.VMEM((TOKENS, D), BF), *sums(), DMA((4,)), DMA((2, 1)), *Reduce.scratch(),
         ],
         compiler_params=params(3),
         name="backward",
@@ -784,7 +794,7 @@
         in_specs=[part, part, down] + [side, side, deep] * 3,
         out_specs=[side, side, deep] * 3,
         out_shape=[jax.ShapeDtypeStruct(x.shape, x.dtype) for x in arrays],
-        compiler_params=pltpu.CompilerParams(vmem_limit_bytes=66_000_000, dimension_semantics=("arbitrary",)),
+        compiler_params=pltpu.CompilerParams(vmem_limit_bytes=67_000_000, dimension_semantics=("arbitrary",)),
         name="update",
     )(*sums_, *arrays)
 
@@ -795,8 +805,8 @@
     def step(x, dy, *arrays):
         x, dy, weights = x[0], dy[0], arrays[:3]
         g0, u0, a0, h1, n1, dys, *f = forward(x, dy, weights)
-        dao, dar, *rest = middle(dys, n1, f, weights)
-        return update(backward(g0, u0, a0, f[2], (dao, dar, h1, dy), rest[3:], rest[:3]), arrays)
+        dh, _, *rest = middle(dys, h1, n1, f, weights)
+        return update(backward(g0, u0, a0, f[2], dh, rest[3:], rest[:3]), arrays)
 
     states, cut = P(AXES, None, None), P(None, ("x", "core"), None)
     return jax.shard_map(

time: 456 us -> 443 us (0.971)
  Pallas kernels: 455 us -> 440 us
    pallas_call x1, Pallas kernels: 149 us -> 134 us  [backward(): pl.pallas_call(back_kernel, grid=(CHUNKS * TILES,), in_specs=blocks + [AN...]
    pallas_call x1, Pallas kernels: 170 us -> 174 us  [middle(): pl.pallas_call(middle_kernel, grid=(CHUNKS * TILES,), in_specs=[pl.BlockS...]
    pallas_call x1, Pallas kernels: 112 us -> 108 us  [forward(): pl.pallas_call(forward_kernel, grid=(steps,), in_specs=[ANY] * 5, out_spe...]
where the time goes in v4:
time: 443 us; the launch traced here: 441 us
  Pallas kernels  440 us (99%)
    pallas_call x1, Pallas kernels, middle(): pl.pallas_call(middle_kernel, grid=(CHUNKS * TILES,), in_specs=[pl.BlockS...  174 us
    pallas_call x1, Pallas kernels, backward(): pl.pallas_call(back_kernel, grid=(CHUNKS * TILES,), in_specs=blocks + [AN...  134 us
    pallas_call x1, Pallas kernels, forward(): pl.pallas_call(forward_kernel, grid=(steps,), in_specs=[ANY] * 5, out_spe...  108 us
    pallas_call x1, Pallas kernels, update(): pl.pallas_call(update_kernel, grid=(SLOTS,), in_specs=[part, part, down]...  24.4 us

profile of v4, /device:TPU:1, one launch (start us, length us, event | category | flops | bytes accessed | tf_op | source)
XLA Modules:
  0.0 440.9 jit_solution(9350043717317987786)
XLA Ops:
  0.6 107.6 %forward.1 = (f32[4,4096,512]{2,1,0:T(8,128)}, f32[4,4096,512]{2,1,0:T(8,128)}, bf16[4096,1024]{1,0:T(8,128)(2,1)}, bf16[2048,1024]{1,0:T(8,128)(2,1)}, bf16[204...) custom-call(bf16[2048,1024]{1,0:T(8,128)(2,1)} %bitcast.2, ...), custom_call_target="tpu_custom_call" | custom-call | tf_op jit(solution)/shard_map/forward/pallas_call | solution.py:452
  108.2 174.3 %middle.1 = (bf16[2048,1024]{1,0:T(8,128)(2,1)}, f32[2048,1024]{1,0:T(8,128)}, bf16[8,2,4,4,32,128]{5,4,3,2,1,0:T(8,128)(2,1)}, bf16[8,2,4,4,32,128]{5,4,3,2,1,0...) custom-call(bf16[4096,1024]{1,0:T(8,128)(2,1)} %get-tuple-element.32, ...), custom_call_target="tpu_custom_call" | custom-call | tf_op jit(solution)/shard_map/middle/pallas_call | solution.py:637
  282.5 133.7 %backward.1 = (bf16[8,2,4,4,32,128]{5,4,3,2,1,0:T(8,128)(2,1)}, bf16[8,2,4,4,32,128]{5,4,3,2,1,0:T(8,128)(2,1)}, bf16[8,128,1024]{2,1,0:T(8,128)(2,1)}) custom-call(f32[4,4096,512]{2,1,0:T(8,128)} %get-tuple-element.28.g_in, f32[4,4096,512]{2,1,0:T(8,128)} %get-tuple-element.29.u_in, ...), custom_call_target="tpu_custom_call", output_to_operand_aliasing={{0}: (8, {}), {1}: (9, {}), {2}: (10, {})} | custom-call | tf_op jit(solution)/shard_map/backward/pallas_call | solution.py:755
  416.3 24.4 %update.1 = (bf16[2,128,4096]{2,1,0:T(8,128)(2,1)}, bf16[2,128,4096]{2,1,0:T(8,128)(2,1)}, bf16[2,512,1024]{2,1,0:T(8,128)(2,1)}, f32[2,128,4096]{2,1,0:T(8,128)...) custom-call(bf16[8,2,4,4,32,128]{5,4,3,2,1,0:T(8,128)(2,1)} %get-tup, ...), custom_call_target="tpu_custom_call" | custom-call | tf_op jit(solution)/shard_map/update/pallas_call | solution.py:791

commit v5 on v4

--- a/solution.py
+++ b/solution.py
@@ -92,16 +92,24 @@
     return sems.at[(0, *at)], sems.at[(1, *at)]
 
 
+def wait_for(whole, sem):
+    pltpu.make_async_copy(whole, whole, sem).wait()
+
+
 class Gather:
-    BASE = (0, 14, 17, 23)
-    SEMS = 29
+    SEMS = 5
 
     def __init__(self, me, w, f, sems):
         self.me, (self.wg, self.wu, self.wd), (self.gf, self.uf, self.df), (self.ss, self.rs, self.ls) = me, w, f, sems
 
-    def _go(self, act, q, base, copies):
-        for n, (src, dst, to) in enumerate(copies, self.BASE[base]):
-            act(remote(src, dst, self.ss.at[q, n], self.rs.at[q, n], to))
+    def _go(self, act, q, n, whole, copies):
+        sems = self.ss.at[q, n], self.rs.at[q, n]
+        if act is START:
+            for src, dst, to in copies:
+                remote(src, dst, *sems, to).start()
+        else:
+            for sem in sems:
+                wait_for(whole, sem)
 
     def first(self, act, l, k, slot, q):
         me = self.me
@@ -111,24 +119,27 @@
         def cols(c):
             return block((me.y * 2 + c) * CHUNKS + k, LANES)
 
-        self._go(act, q, 0, [(w.at[l, rows, cols(lax.rem(me.core + dc, 2))], to, me.plus(x=dx, core=dc)) for dx, dc in ROW for w, to in both])
+        whole = self.gf.at[slot, 0, pl.ds(0, len(ROW)), pl.ds(0, 2)]
+        self._go(act, q, 0, whole, [(w.at[l, rows, cols(lax.rem(me.core + dc, 2))], to, me.plus(x=dx, core=dc)) for dx, dc in ROW for w, to in both])
         for i, (w, to) in enumerate(both):
             act(pltpu.make_async_copy(w.at[l, rows, cols(me.core)], to, self.ls.at[q, i]))
 
     def down(self, act, l, k, slot, q):
         src, dst = self.wd.at[l, block(k, LANES)], self.df.at[slot, self.me.x]
-        self._go(act, q, 1, [(src, dst, self.me.plus(x=d)) for d in OTHERS])
+        self._go(act, q, 1, self.df.at[slot, pl.ds(0, 3)], [(src, dst, self.me.plus(x=d)) for d in OTHERS])
         act(pltpu.make_async_copy(src, dst, self.ls.at[q, 2]))
 
     def second(self, act, slot, q):
         me = self.me
         g, u = (f.at[slot, me.y, :, me.z] for f in (self.gf, self.uf))
-        self._go(act, q, 2, [c for d in OTHERS for c in ((g, g, me.plus(y=d)), (u, u, me.plus(z=d)))])
+        whole = self.gf.at[slot, pl.ds(0, 3), :, pl.ds(0, 2)]
+        self._go(act, q, 2, whole, [c for d in OTHERS for c in ((g, g, me.plus(y=d)), (u, u, me.plus(z=d)))])
 
     def third(self, act, slot, q):
         me = self.me
         g, u = self.gf.at[slot, :, :, me.z], self.uf.at[slot, me.y]
-        self._go(act, q, 3, [c for d in OTHERS for c in ((g, g, me.plus(z=d)), (u, u, me.plus(y=d)))])
+        self._go(act, q, 3, self.gf.at[slot, pl.ds(0, 3)], [(g, g, me.plus(z=d)) for d in OTHERS])
+        self._go(act, q, SIDE, self.uf.at[slot, pl.ds(0, 3)], [(u, u, me.plus(y=d)) for d in OTHERS])
 
     def load(self, act, slot, v, sem):
         load(act, (self.gf, self.uf, self.df), slot, v, sem)
@@ -149,8 +160,6 @@
 
 
 class Reduce:
-    BASE = (0, 9, 18, 35)
-
     @staticmethod
     def scratch():
         v = pltpu.VMEM
@@ -164,7 +173,7 @@
             held(8, PART, LANES), held(8, PART, LANES), held(PART, D),
             v((2, 8, PART, LANES), BF), v((2, 8, PART, LANES), BF), came(PART, QUARTER),
             held(2, 2, PART, LANES), held(2, 2, PART, LANES), held(2, PART, QUARTER),
-            DMA((2, 44)), DMA((2, 44)), DMA((SIDE, 9)), DMA((SIDE, 9)), DMA((2, 3)),
+            DMA((2, SIDE, 3)), DMA((2, SIDE, 3)), DMA((SIDE, 3)), DMA((SIDE, 3)), DMA((2, 3)),
         ]
 
     def __init__(self, me, scratch, out):
@@ -212,14 +221,24 @@
                 yield u.at[slot, :, :, me.z], u.at[slot, :, :, me.z], me.plus(z=by)
                 yield d.at[slot, :, col], d.at[slot, :, col], me.plus(z=by)
 
+    def sems(self, stage, slot, q, i):
+        if stage > SIDE:
+            return self.sl.at[slot % SIDE, i], self.rl.at[slot % SIDE, i]
+        return self.ss.at[q, stage - 1, i], self.rs.at[q, stage - 1, i]
+
     def send(self, stage, act, slot, q):
         me = self.me
-        for n, (src, dst, to) in enumerate(self.copies(stage, slot, q)):
-            if stage > SIDE:
-                act(remote(src, dst, self.sl.at[slot % SIDE, n], self.rl.at[slot % SIDE, n], to))
-            else:
-                n += self.BASE[stage - 1]
-                act(remote(src, dst, self.ss.at[q, n], self.rs.at[q, n], to))
+        if act is START:
+            for n, (src, dst, to) in enumerate(self.copies(stage, slot, q)):
+                i = n % 3 if stage != 3 else n % 2 if n < 2 * len(ROW) else 2
+                remote(src, dst, *self.sems(stage, slot, q, i), to).start()
+        else:
+            for i in range(3):
+                whole = (self.r1, self.r2, self.r3, self.r3, self.r2)[stage - 1][i].at[q]
+                if stage in (3, SIDE) and i < 2:
+                    whole = self.r3[i].at[q, pl.ds(0, len(ROW) if stage == 3 else 6)]
+                for sem in self.sems(stage, slot, q, i):
+                    wait_for(whole, sem)
         if stage == SIDE:
             g, u, d = self.out
             ends = g.at[slot, :, me.y, me.z], u.at[slot, :, me.y, me.z], d.at[slot, block(me.y, PART), block(me.z, QUARTER)]

time: 443 us -> 437 us (0.986)
  no operation moved by 1% of the time
where the time goes in v5:
time: 437 us
  Pallas kernels  436 us (100%)
    pallas_call x1, Pallas kernels, middle(): pl.pallas_call(middle_kernel, grid=(CHUNKS * TILES,), in_specs=[pl.BlockS...  170 us
    pallas_call x1, Pallas kernels, backward(): pl.pallas_call(back_kernel, grid=(CHUNKS * TILES,), in_specs=blocks + [AN...  136 us
    pallas_call x1, Pallas kernels, forward(): pl.pallas_call(forward_kernel, grid=(steps,), in_specs=[ANY] * 5, out_spe...  105 us
    pallas_call x1, Pallas kernels, update(): pl.pallas_call(update_kernel, grid=(SLOTS,), in_specs=[part, part, down]...  24.4 us

profile of v5, /device:TPU:1, one launch (start us, length us, event | category | flops | bytes accessed | tf_op | source)
XLA Modules:
  0.0 436.7 jit_solution(16554450950160197356)
XLA Ops:
  0.6 105.2 %forward.1 = (f32[4,4096,512]{2,1,0:T(8,128)}, f32[4,4096,512]{2,1,0:T(8,128)}, bf16[4096,1024]{1,0:T(8,128)(2,1)}, bf16[2048,1024]{1,0:T(8,128)(2,1)}, bf16[204...) custom-call(bf16[2048,1024]{1,0:T(8,128)(2,1)} %bitcast.2, ...), custom_call_target="tpu_custom_call" | custom-call | tf_op jit(solution)/shard_map/forward/pallas_call | solution.py:471
  105.8 170.1 %middle.1 = (bf16[2048,1024]{1,0:T(8,128)(2,1)}, f32[2048,1024]{1,0:T(8,128)}, bf16[8,2,4,4,32,128]{5,4,3,2,1,0:T(8,128)(2,1)}, bf16[8,2,4,4,32,128]{5,4,3,2,1,0...) custom-call(bf16[4096,1024]{1,0:T(8,128)(2,1)} %get-tuple-element.32, ...), custom_call_target="tpu_custom_call" | custom-call | tf_op jit(solution)/shard_map/middle/pallas_call | solution.py:656
  276.0 136.1 %backward.1 = (bf16[8,2,4,4,32,128]{5,4,3,2,1,0:T(8,128)(2,1)}, bf16[8,2,4,4,32,128]{5,4,3,2,1,0:T(8,128)(2,1)}, bf16[8,128,1024]{2,1,0:T(8,128)(2,1)}) custom-call(f32[4,4096,512]{2,1,0:T(8,128)} %get-tuple-element.28.g_in, f32[4,4096,512]{2,1,0:T(8,128)} %get-tuple-element.29.u_in, ...), custom_call_target="tpu_custom_call", output_to_operand_aliasing={{0}: (8, {}), {1}: (9, {}), {2}: (10, {})} | custom-call | tf_op jit(solution)/shard_map/backward/pallas_call | solution.py:774
  412.1 24.4 %update.1 = (bf16[2,128,4096]{2,1,0:T(8,128)(2,1)}, bf16[2,128,4096]{2,1,0:T(8,128)(2,1)}, bf16[2,512,1024]{2,1,0:T(8,128)(2,1)}, f32[2,128,4096]{2,1,0:T(8,128)...) custom-call(bf16[8,2,4,4,32,128]{5,4,3,2,1,0:T(8,128)(2,1)} %get-tup, ...), custom_call_target="tpu_custom_call" | custom-call | tf_op jit(solution)/shard_map/update/pallas_call | solution.py:810

commit v6 on v5

--- a/solution.py
+++ b/solution.py
@@ -42,10 +42,23 @@
     return lax.dot_general(a, b, (((0,), (0,)), ((), ())), preferred_element_type=F32)
 
 
+def mean(rows):
+    return jnp.mean(rows, -1, keepdims=True)
+
+
+def scale_of(wide):
+    return lax.rsqrt(mean(wide * wide) + 1e-6)
+
+
 def normed(h):
     wide = h.astype(F32)
-    scale = lax.rsqrt(jnp.mean(wide**2, -1, keepdims=True) + 1e-6)
-    return (wide * scale).astype(BF)
+    return (wide * scale_of(wide)).astype(BF)
+
+
+def norm_back(h, by_a):
+    wide, g = h.astype(F32), by_a.astype(F32)
+    s = scale_of(wide)
+    return (s * g - wide * (s * s * s * mean(g * wide))).astype(BF)
 
 
 def sigmoid(g):
@@ -339,10 +352,10 @@
         fetch = pltpu.make_async_copy(x, xv, csem.at[1])
         fetch.start()
         greet(me)
-        spread(0, START, "first")
-        spread(1, START, "first")
+        for m in range(3):
+            spread(m, START, "first")
         spread(0, START, "down")
-        for m in range(2, CHUNKS + 1):
+        for m in range(3, CHUNKS + 1):
             spread(m, START, "first")
         spread(1, START, "down")
         fetch.wait()
@@ -362,11 +375,11 @@
         spread(0, START, "third")
         spread(2, WAIT, "first")
         spread(2, START, "second")
+        spread(1, WAIT, "second")
+        spread(1, START, "third")
         spread(0, WAIT, "third")
         spread(0, WAIT, "down")
         save_d.start()
-        spread(1, WAIT, "second")
-        spread(1, START, "third")
 
     @when(t == 0)
     def _():
@@ -559,13 +572,14 @@
     @when(i == MINE)
     def _():
         to_a.wait()
-        for c in range(last):
-            bring("second", WAIT, c)
+        bring("second", WAIT, 0)
         bring("third", START, 0)
         bring("down", START, 1)
 
     @when(i == TILES - 1)
     def _():
+        for c in range(1, last):
+            bring("second", WAIT, c)
         bring("third", START, 1)
 
     @when(i == TILES + 1)
@@ -637,7 +651,7 @@
 
             piece(WAIT, j)
             r, s = block(j, LANES), j % SIDE
-            by_h = jax.vjp(normed, vd[0, s])[1]((da[r] + ad[block(s, LANES)]).astype(BF))[0]
+            by_h = norm_back(vd[0, s], (da[r] + ad[block(s, LANES)]).astype(BF))
             a[r] = (vd[1, s].astype(F32) + by_h.astype(F32)).astype(BF)
             pltpu.make_async_copy(a.at[r], dh.at[r], csem.at[0]).start()
             return 0
@@ -753,8 +767,8 @@
         q, p = CHUNKS % 2, 1 - CHUNKS % 2
         re.send(1, START, end, q)
         re.send(5, WAIT, end - 3, p)
+        re.turn(2, end - 1, p)
         re.turn(4, end - 2, q)
-        re.turn(2, end - 1, p)
         re.turn(1, end, q)
         re.turn(3, end - 1, p)
         re.turn(2, end, q)

time: 437 us -> 433 us (level)
  Pallas kernels: 436 us -> 431 us
where the time goes in v6:
time: 433 us; the launch traced here: 432 us
  Pallas kernels  431 us (100%)
    pallas_call x1, Pallas kernels, middle(): pl.pallas_call(middle_kernel, grid=(CHUNKS * TILES,), in_specs=[pl.BlockS...  169 us
    pallas_call x1, Pallas kernels, backward(): pl.pallas_call(back_kernel, grid=(CHUNKS * TILES,), in_specs=blocks + [AN...  134 us
    pallas_call x1, Pallas kernels, forward(): pl.pallas_call(forward_kernel, grid=(steps,), in_specs=[ANY] * 5, out_spe...  103 us
    pallas_call x1, Pallas kernels, update(): pl.pallas_call(update_kernel, grid=(SLOTS,), in_specs=[part, part, down]...  24.4 us

profile of v6, /device:TPU:1, one launch (start us, length us, event | category | flops | bytes accessed | tf_op | source)
XLA Modules:
  0.0 432.0 jit_solution(4827825507236209208)
XLA Ops:
  0.6 103.0 %forward.1 = (f32[4,4096,512]{2,1,0:T(8,128)}, f32[4,4096,512]{2,1,0:T(8,128)}, bf16[4096,1024]{1,0:T(8,128)(2,1)}, bf16[2048,1024]{1,0:T(8,128)(2,1)}, bf16[204...) custom-call(bf16[2048,1024]{1,0:T(8,128)(2,1)} %bitcast.2, ...), custom_call_target="tpu_custom_call" | custom-call | tf_op jit(solution)/shard_map/forward/pallas_call | solution.py:484
  103.7 169.5 %middle.1 = (bf16[2048,1024]{1,0:T(8,128)(2,1)}, f32[2048,1024]{1,0:T(8,128)}, bf16[8,2,4,4,32,128]{5,4,3,2,1,0:T(8,128)(2,1)}, bf16[8,2,4,4,32,128]{5,4,3,2,1,0...) custom-call(bf16[4096,1024]{1,0:T(8,128)(2,1)} %get-tuple-element.32, ...), custom_call_target="tpu_custom_call" | custom-call | tf_op jit(solution)/shard_map/middle/pallas_call | solution.py:670
  273.1 134.2 %backward.1 = (bf16[8,2,4,4,32,128]{5,4,3,2,1,0:T(8,128)(2,1)}, bf16[8,2,4,4,32,128]{5,4,3,2,1,0:T(8,128)(2,1)}, bf16[8,128,1024]{2,1,0:T(8,128)(2,1)}) custom-call(f32[4,4096,512]{2,1,0:T(8,128)} %get-tuple-element.28.g_in, f32[4,4096,512]{2,1,0:T(8,128)} %get-tuple-element.29.u_in, ...), custom_call_target="tpu_custom_call", output_to_operand_aliasing={{0}: (8, {}), {1}: (9, {}), {2}: (10, {})} | custom-call | tf_op jit(solution)/shard_map/backward/pallas_call | solution.py:788
  407.4 24.4 %update.1 = (bf16[2,128,4096]{2,1,0:T(8,128)(2,1)}, bf16[2,128,4096]{2,1,0:T(8,128)(2,1)}, bf16[2,512,1024]{2,1,0:T(8,128)(2,1)}, f32[2,128,4096]{2,1,0:T(8,128)...) custom-call(bf16[8,2,4,4,32,128]{5,4,3,2,1,0:T(8,128)(2,1)} %get-tup, ...), custom_call_target="tpu_custom_call" | custom-call | tf_op jit(solution)/shard_map/update/pallas_call | solution.py:824

commit v7 on v6

--- a/solution.py
+++ b/solution.py
@@ -26,6 +26,7 @@
 START, WAIT = (lambda c: c.start()), (lambda c: c.wait())
 LANES, PART, QUARTER, SLOTS = 128, 32, 256, 8
 PIECES = OWN // QUARTER
+PAIR, UNITS = 2, 3
 SLICED = (SIDE, 8, SIDE, PART, LANES)
 BLOCKS = (SIDE, LANES, D)
 
@@ -177,16 +178,16 @@
     def scratch():
         v = pltpu.VMEM
         held = lambda *s: v(s, BF)
-        came = lambda *s: v((2, 3) + s, BF)
+        came = lambda *s: v((PAIR, UNITS) + s, BF)
         return [
             held(*SLICED), held(*SLICED), held(*BLOCKS),
             came(8, SIDE, PART, LANES), came(SIDE, 8, PART, LANES), came(LANES, D),
             held(8, SIDE, PART, LANES), held(SIDE, 8, PART, LANES), held(LANES, D),
             came(8, PART, LANES), came(8, PART, LANES), came(PART, D),
             held(8, PART, LANES), held(8, PART, LANES), held(PART, D),
-            v((2, 8, PART, LANES), BF), v((2, 8, PART, LANES), BF), came(PART, QUARTER),
-            held(2, 2, PART, LANES), held(2, 2, PART, LANES), held(2, PART, QUARTER),
-            DMA((2, SIDE, 3)), DMA((2, SIDE, 3)), DMA((SIDE, 3)), DMA((SIDE, 3)), DMA((2, 3)),
+            v((PAIR, 8, PART, LANES), BF), v((PAIR, 8, PART, LANES), BF), came(PART, QUARTER),
+            held(PAIR, PAIR, PART, LANES), held(PAIR, PAIR, PART, LANES), held(PAIR, PART, QUARTER),
+            DMA((PAIR, SIDE, UNITS)), DMA((PAIR, SIDE, UNITS)), DMA((SIDE, UNITS)), DMA((SIDE, UNITS)), DMA((PAIR, UNITS)),
         ]
 
     def __init__(self, me, scratch, out):
@@ -809,21 +810,27 @@
 
 def update_kernel(gg, gu, gd, *refs):
     ins, outs = refs[:9], refs[9:]
-    sides = [jnp.concatenate([r[k, c, 0].reshape(LANES, LANES) for c in range(2) for k in range(CHUNKS)], axis=1) for r in (gg, gu)]
-    for n, g in enumerate((*sides, gd[0])):
-        w, m, v = (r[0] for r in ins[n::3])
+
+    def one(n, at, g):
+        w, m, v = (r[at] for r in ins[n::3])
         for out, new in zip(outs[n::3], adamw(w.astype(F32), m, v, g.astype(F32))):
-            out[0] = new
+            out[at] = new
+
+    for u in range(2):
+        for n, r in enumerate((gg, gu)):
+            g = jnp.concatenate([r[k, c, u].reshape(LANES, LANES) for c in range(2) for k in range(CHUNKS)], axis=1)
+            one(n, (0, slice(None), slice(u * D, u * D + D)), g)
+        one(2, (0, slice(u * LANES, u * LANES + LANES)), gd[u])
 
 
 def update(sums_, arrays):
-    side = pl.BlockSpec((1, LANES, D), lambda i: (i // SIDE, 0, i % SIDE))
-    deep = pl.BlockSpec((1, LANES, D), lambda i: (i // SIDE, i % SIDE, 0))
-    part = pl.BlockSpec((CHUNKS, 2, 1, SIDE, PART, LANES), lambda i: (1 - i // SIDE, 0, i % SIDE, 0, 0, 0))
-    down = pl.BlockSpec((1, LANES, D), lambda i: ((1 - i // SIDE) * CHUNKS + i % SIDE, 0, 0))
+    side = pl.BlockSpec((1, LANES, 2 * D), lambda i: (i // 2, 0, i % 2))
+    deep = pl.BlockSpec((1, 2 * LANES, D), lambda i: (i // 2, i % 2, 0))
+    part = pl.BlockSpec((CHUNKS, 2, 2, SIDE, PART, LANES), lambda i: (1 - i // 2, 0, i % 2, 0, 0, 0))
+    down = pl.BlockSpec((2, LANES, D), lambda i: (2 - i // 2 * 2 + i % 2, 0, 0))
     return pl.pallas_call(
         update_kernel,
-        grid=(SLOTS,),
+        grid=(SIDE,),
         in_specs=[part, part, down] + [side, side, deep] * 3,
         out_specs=[side, side, deep] * 3,
         out_shape=[jax.ShapeDtypeStruct(x.shape, x.dtype) for x in arrays],

time: 433 us -> 431 us (level)
  no operation moved by 1% of the time
where the time goes in v7:
time: 431 us; the launch traced here: 430 us
  Pallas kernels  429 us (100%)
    pallas_call x1, Pallas kernels, middle(): pl.pallas_call(middle_kernel, grid=(CHUNKS * TILES,), in_specs=[pl.BlockS...  169 us
    pallas_call x1, Pallas kernels, backward(): pl.pallas_call(back_kernel, grid=(CHUNKS * TILES,), in_specs=blocks + [AN...  134 us
    pallas_call x1, Pallas kernels, forward(): pl.pallas_call(forward_kernel, grid=(steps,), in_specs=[ANY] * 5, out_spe...  103 us
    pallas_call x1, Pallas kernels, update(): pl.pallas_call(update_kernel, grid=(SIDE,), in_specs=[part, part, down] +...  22 us

profile of v7, /device:TPU:1, one launch (start us, length us, event | category | flops | bytes accessed | tf_op | source)
XLA Modules:
  0.0 429.5 jit_solution(11663254335162775144)
XLA Ops:
  0.6 103.0 %forward.1 = (f32[4,4096,512]{2,1,0:T(8,128)}, f32[4,4096,512]{2,1,0:T(8,128)}, bf16[4096,1024]{1,0:T(8,128)(2,1)}, bf16[2048,1024]{1,0:T(8,128)(2,1)}, bf16[204...) custom-call(bf16[2048,1024]{1,0:T(8,128)(2,1)} %bitcast.2, ...), custom_call_target="tpu_custom_call" | custom-call | tf_op jit(solution)/shard_map/forward/pallas_call | solution.py:485
  103.7 169.5 %middle.1 = (bf16[2048,1024]{1,0:T(8,128)(2,1)}, f32[2048,1024]{1,0:T(8,128)}, bf16[8,2,4,4,32,128]{5,4,3,2,1,0:T(8,128)(2,1)}, bf16[8,2,4,4,32,128]{5,4,3,2,1,0...) custom-call(bf16[4096,1024]{1,0:T(8,128)(2,1)} %get-tuple-element.32, ...), custom_call_target="tpu_custom_call" | custom-call | tf_op jit(solution)/shard_map/middle/pallas_call | solution.py:671
  273.1 134.2 %backward.1 = (bf16[8,2,4,4,32,128]{5,4,3,2,1,0:T(8,128)(2,1)}, bf16[8,2,4,4,32,128]{5,4,3,2,1,0:T(8,128)(2,1)}, bf16[8,128,1024]{2,1,0:T(8,128)(2,1)}) custom-call(f32[4,4096,512]{2,1,0:T(8,128)} %get-tuple-element.28.g_in, f32[4,4096,512]{2,1,0:T(8,128)} %get-tuple-element.29.u_in, ...), custom_call_target="tpu_custom_call", output_to_operand_aliasing={{0}: (8, {}), {1}: (9, {}), {2}: (10, {})} | custom-call | tf_op jit(solution)/shard_map/backward/pallas_call | solution.py:789
  407.4 22.0 %update.1 = (bf16[2,128,4096]{2,1,0:T(8,128)(2,1)}, bf16[2,128,4096]{2,1,0:T(8,128)(2,1)}, bf16[2,512,1024]{2,1,0:T(8,128)(2,1)}, f32[2,128,4096]{2,1,0:T(8,128)...) custom-call(bf16[8,2,4,4,32,128]{5,4,3,2,1,0:T(8,128)(2,1)} %get-tup, ...), custom_call_target="tpu_custom_call" | custom-call | tf_op jit(solution)/shard_map/update/pallas_call | solution.py:831
